TPU v7x, 128 devices: a whole 4x4x4 slice. The times are simulated.
128 devices in a mesh: chain: 8 (over x, core), quad: 16 (over z, y).
Axes of the slice: x: 4, y: 4, z: 4, core: 2. Of those that a mesh axis runs over, the one named last changes fastest.
Arguments:
- sections: bfloat16 [8, 4096, 4096], P('chain', 'quad'), may hold values from -8 to 8
- anchor: bfloat16 [4096, 4096], P('quad'), may hold values from -8 to 8
Outputs:
- registered: bfloat16 [8, 4096, 4096], P('chain', 'quad')
- accumulated: float32 [8, 64, 128], P('chain')
All inputs are finite; a program needn't handle non-finite values.
Results may differ from a plain program's by a relative error of at most 0.00135.
The roundings to bfloat16 on the way count: a program that leaves them out, or rounds other values in their place, can miss the bound.
Values may be sent and summed in bfloat16 or wider, within the bound.
A program may use at most 128 MiB of HBM per device.

v0:
```python
import numpy as np
import jax
import jax.numpy as jnp
from jax import lax
from jax.experimental import pallas as pl
from jax.experimental.pallas import tpu as pltpu
from jax.sharding import PartitionSpec as P

GRID = 64
ITERATIONS = 4
EPS = 1e-6
SMOOTHING = 0.25
MESH = pl.DeviceIdType.MESH
F32 = jnp.float32
BF16 = jnp.bfloat16

ROWS = 256
COLS = 4096
HALF = 128
CH = 256
NCH = COLS // CH
PAD = 128
NC = 8
NQ = 16
PIXELS = float(4096 * 4096)


def weight(offset):
    d = np.abs(offset)
    near = 2.0 / 3.0 - d * d + 0.5 * d * d * d
    r = 2.0 - d
    far = r * r * r / 6.0
    return np.where(d < 1.0, near, np.where(d < 2.0, far, 0.0 * d)).astype(np.float32)


def bf(x):
    return np.asarray(jnp.asarray(x, jnp.float32).astype(BF16).astype(jnp.float32))


def hi_lo(x):
    hi = bf(x)
    return [hi, bf(x - hi)]


def tables():
    f = np.float32
    x = np.arange(COLS, dtype=f)
    c = weight((x[:, None] + f(0.5)) / f(64) - np.arange(GRID, dtype=f)[None, :] - f(0.5))
    c = np.concatenate([c, c], axis=1)
    y = np.arange(-1, ROWS + 1, dtype=f)
    ext = weight((y[:, None] + f(0.5)) / f(64) - (np.arange(8, dtype=f) - f(2))[None, :] - f(0.5)).T
    r = ext[:, 1:-1]
    pairs = np.zeros((4, 8, ROWS), f)
    for d in range(4):
        pairs[d, : 8 - d] = r[: 8 - d] * r[d:]
    step = 0.5 * (r - ext[:, 2:])
    rows = []
    for variant in range(3):
        e = ext.copy()
        if variant == 0:
            e[:, 0] = 0.0
        if variant == 2:
            e[:, -1] = 0.0
        slope = 0.5 * (e[:, :-2] - e[:, 2:])
        rows.append(np.concatenate([pairs.reshape(32, ROWS)] + hi_lo(r) + hi_lo(slope) + hi_lo(step), axis=0))
    top = (np.arange(ROWS) < HALF).astype(f)[None]
    split = np.concatenate([h * top for h in hi_lo(r)] + [h * (1 - top) for h in hi_lo(r)], axis=0)
    hi = bf(r)
    mid = bf(r - hi)
    low = bf(r - hi - mid)
    mix = np.concatenate([hi, hi, hi, mid, mid, low, np.zeros((80, ROWS), f)], axis=0).T
    return c, np.stack(rows), split, mix


def kernel(
    sec, anc, cd_in, rt_in, sp_in, mx_in,
    reg, acc,
    ib, fb, jb, ab, i32, j32, lxb, lyb, cd, w1, rt, sp, mx,
    qb, qd, tg, ub, lhs, bdacc, sums, dsums,
    etop, ebot, emid, htop, hbot, jmid, jbot,
    gfs, gbs, gf, gb, ga, gx, bds, bhs, bdo, bdh,
    cpad, csend, cprev, cnext, ew_s, ew, tw_s, tw,
    sem_in, sem_c, sem_a,
    s_f, r_f, s_j, r_j, s_h, r_h, s_gf, r_gf, s_gb, r_gb,
    s_bo, r_bo, s_bh, r_bh, s_cp, r_cp, s_cn, r_cn, s_ew, r_ew, s_tw, r_tw,
):
    k = lax.axis_index("chain")
    s = lax.axis_index("quad")
    has_prev = k > 0
    has_next = k < NC - 1

    def remote(src, dst, ss, rs, kk, qq):
        return pltpu.make_async_remote_copy(
            src_ref=src, dst_ref=dst, send_sem=ss, recv_sem=rs,
            device_id={"chain": kk, "quad": qq}, device_id_type=MESH,
        )

    def in_copy(c):
        w = COLS // 4
        return pltpu.make_async_copy(
            sec.at[0, :, pl.ds(c * w, w)], ib.at[:, pl.ds(c * w, w)], sem_in.at[c]
        )

    for c in range(4):
        in_copy(c).start()
    consts = [
        pltpu.make_async_copy(cd_in, cd, sem_c.at[0]),
        pltpu.make_async_copy(rt_in, rt, sem_c.at[1]),
        pltpu.make_async_copy(sp_in, sp, sem_c.at[2]),
        pltpu.make_async_copy(mx_in, mx, sem_c.at[3]),
    ]
    for d in consts:
        d.start()
    anc_copies = [
        pltpu.make_async_copy(anc.at[pl.ds(0, HALF)], fb, sem_a.at[0]),
        pltpu.make_async_copy(anc.at[pl.ds(HALF, HALF)], ab, sem_a.at[1]),
    ]

    @pl.when(k == 0)
    def _():
        for d in anc_copies:
            d.start()

    barrier = pltpu.get_barrier_semaphore()

    def hello(kk, qq):
        pl.semaphore_signal(barrier, inc=1, device_id={"chain": kk, "quad": qq}, device_id_type=MESH)

    @pl.loop(1, NQ)
    def _(d):
        hello(k, lax.rem(s + d, NQ))

    @pl.loop(0, NQ)
    def _(q):
        @pl.when(has_next)
        def _():
            hello(k + 1, q)

        @pl.when(has_prev)
        def _():
            hello(k - 1, q)

    @pl.loop(0, NC)
    def _(kk):
        @pl.when((kk > k + 1) | (kk < k - 1))
        def _():
            hello(kk, s)

    one = jnp.int32(1)
    zero = jnp.int32(0)
    nn = jnp.where(has_next, one, zero)
    np_ = jnp.where(has_prev, one, zero)
    partners = (NQ - 1) + NQ * nn + NQ * np_ + (NC - 1) - nn - np_

    i32[:, :PAD] = jnp.zeros((ROWS + 16, PAD), F32)
    i32[:, PAD + COLS :] = jnp.zeros((ROWS + 16, PAD), F32)
    j32[:, :PAD] = jnp.zeros((HALF + 16, PAD), F32)
    j32[:, PAD + COLS :] = jnp.zeros((HALF + 16, PAD), F32)
    ub[:, :PAD] = jnp.zeros((32, PAD), F32)
    ub[:, PAD + COLS :] = jnp.zeros((32, PAD), F32)
    sums[...] = jnp.zeros_like(sums)
    dsums[...] = jnp.zeros_like(dsums)
    bdacc[...] = jnp.zeros_like(bdacc)
    cpad[...] = jnp.zeros_like(cpad)

    @pl.when(s == 0)
    def _():
        htop[...] = jnp.zeros_like(htop)

    @pl.when(s == NQ - 1)
    def _():
        hbot[...] = jnp.zeros_like(hbot)

    @pl.when(k == 0)
    def _():
        bdh[...] = jnp.zeros_like(bdh)
        cprev[...] = jnp.zeros_like(cprev)

    @pl.when(k == NC - 1)
    def _():
        jb[...] = jnp.zeros_like(jb)
        jmid[...] = jnp.zeros_like(jmid)
        jbot[...] = jnp.zeros_like(jbot)
        cnext[...] = jnp.zeros_like(cnext)

    for j in range(NC - 1):
        @pl.when(j >= k)
        def _():
            ew[j] = jnp.zeros((8, 128), F32)

    for c in range(4):
        in_copy(c).wait()

    @pl.loop(0, NCH)
    def _(c):
        at = pl.multiple_of(c * CH, CH)
        i32[8 : 8 + ROWS, pl.ds(at + PAD, CH)] = ib[:, pl.ds(at, CH)].astype(F32)

    etop[...] = i32[8:9, PAD : PAD + COLS]
    ebot[...] = i32[7 + ROWS : 8 + ROWS, PAD : PAD + COLS]
    emid[...] = i32[7 + HALF : 8 + HALF, PAD : PAD + COLS]

    pl.semaphore_wait(barrier, partners)

    up_top = remote(etop, hbot, s_h.at[0], r_h.at[0], k, jnp.maximum(s - 1, 0))
    down_bot = remote(ebot, htop, s_h.at[1], r_h.at[1], k, jnp.minimum(s + 1, NQ - 1))
    mid_prev = remote(emid, jmid, s_h.at[2], r_h.at[2], jnp.maximum(k - 1, 0), s)
    bot_prev = remote(hbot, jbot, s_h.at[3], r_h.at[3], jnp.maximum(k - 1, 0), s)

    @pl.when(s > 0)
    def _():
        up_top.start()

    @pl.when(s < NQ - 1)
    def _():
        down_bot.start()

    def f_copy(c):
        at = pl.multiple_of(c * CH, CH)
        return remote(
            ib.at[pl.ds(0, HALF), pl.ds(at, CH)], fb.at[:, pl.ds(at, CH)],
            s_f.at[c], r_f.at[c], jnp.minimum(k + 1, NC - 1), s,
        )

    def j_copy(c):
        at = pl.multiple_of(c * CH, CH)
        return remote(
            ib.at[pl.ds(HALF, HALF), pl.ds(at, CH)], jb.at[:, pl.ds(at, CH)],
            s_j.at[c], r_j.at[c], jnp.maximum(k - 1, 0), s,
        )

    @pl.when(has_prev)
    def _():
        mid_prev.start()

    @pl.loop(0, NCH)
    def _(c):
        @pl.when(has_next)
        def _():
            f_copy(c).start()

        @pl.when(has_prev)
        def _():
            j_copy(c).start()

    for d in consts:
        d.wait()
    lane = lax.broadcasted_iota(jnp.int32, (8, 128), 1)

    @pl.loop(0, NCH)
    def _(c):
        at = pl.multiple_of(c * CH, CH)
        v = cd[pl.ds(at, CH), :].astype(F32)
        ln = lax.broadcasted_iota(jnp.int32, (CH, 128), 1)
        j = jnp.where(ln < GRID, ln, ln - GRID)
        for h in range(2):
            lo_d, hi_d = 2 * h, 2 * h + 1
            a = v if lo_d == 0 else pltpu.roll(v, 128 - lo_d, 1)
            b = pltpu.roll(v, 128 - hi_d, 1)
            a = jnp.where(j < GRID - lo_d, a, 0.0)
            b = jnp.where(j < GRID - hi_d, b, 0.0)
            w1[pl.ds(at, CH), h * 128 : (h + 1) * 128] = (v * jnp.where(ln < GRID, a, b)).astype(BF16)

    @pl.when(s < NQ - 1)
    def _():
        up_top.wait_recv()

    @pl.when(s > 0)
    def _():
        down_bot.wait_recv()

    @pl.when(has_prev)
    def _():
        bot_prev.start()

    i32[7:8, PAD : PAD + COLS] = htop[...]
    i32[8 + ROWS : 9 + ROWS, PAD : PAD + COLS] = hbot[...]

    variant = jnp.where(s == 0, 0, jnp.where(s == NQ - 1, 2, 1))
    RB = 32

    @pl.loop(0, NCH)
    def _(c):
        at = pl.multiple_of(c * CH, CH)
        s1 = jnp.zeros((8, CH), F32)
        s2 = jnp.zeros((8, CH), F32)
        for r in range(0, ROWS, RB):
            mid = i32[8 + r : 8 + r + RB, pl.ds(at, CH + 2 * PAD)]
            x = mid[:, PAD : PAD + CH]
            right = pltpu.roll(mid, CH + 2 * PAD - 1, 1)[:, PAD : PAD + CH]
            left = pltpu.roll(mid, 1, 1)[:, PAD : PAD + CH]
            tall = i32[r : r + RB + 16, pl.ds(at + PAD, CH)]
            below = pltpu.roll(tall, RB + 15, 0)[8 : 8 + RB]
            above = pltpu.roll(tall, 1, 0)[8 : 8 + RB]
            lx = right - left
            ly = below - above
            lxb[r : r + RB, pl.ds(at, CH)] = lx
            lyb[r : r + RB, pl.ds(at, CH)] = ly
            qb[0, r : r + RB, :] = (lx * lx).astype(BF16)
            qb[1, r : r + RB, :] = (lx * ly).astype(BF16)
            qb[2, r : r + RB, :] = (ly * ly).astype(BF16)
            qb[3, r : r + RB, :] = (x * right).astype(BF16)
            qb[4, r : r + RB, :] = (x * below).astype(BF16)
            for t in range(0, RB, 8):
                xt = x[t : t + 8]
                s1 = s1 + xt
                s2 = s2 + xt * xt
        sums[0] = sums[0] + s1[:, :128] + s1[:, 128:]
        sums[1] = sums[1] + s2[:, :128] + s2[:, 128:]
        for i in range(3):
            tg[32 * i : 32 * i + 32, pl.ds(at, CH)] = jnp.dot(
                rt[variant, 0:32, :], qb[i], preferred_element_type=F32
            ).astype(BF16)
        u = jnp.dot(rt[variant, 32:64, :], ib[:, pl.ds(at, CH)], preferred_element_type=F32)
        z = jnp.dot(rt[variant, 32:48, :], qb[3], preferred_element_type=F32)
        q = jnp.dot(rt[variant, 64:80, :], qb[4], preferred_element_type=F32)
        ub[0:8, pl.ds(at + PAD, CH)] = u[0:8] + u[8:16]
        ub[8:16, pl.ds(at + PAD, CH)] = u[16:24] + u[24:32]
        ub[16:24, pl.ds(at + PAD, CH)] = z[0:8] + z[8:16]
        ub[24:32, pl.ds(at + PAD, CH)] = q[0:8] + q[8:16]

    g = jnp.dot(tg[...], w1[...], preferred_element_type=F32) * 0.25
    first = lane < GRID

    def swap(v):
        return pltpu.roll(v, GRID, 1)

    fslots = []
    bslots = []
    for di in range(4):
        for h in range(2):
            xx = g[8 * di : 8 * di + 8, 128 * h : 128 * h + 128]
            xy = g[32 + 8 * di : 40 + 8 * di, 128 * h : 128 * h + 128]
            yy = g[64 + 8 * di : 72 + 8 * di, 128 * h : 128 * h + 128]
            a0 = jnp.where(first, xx, swap(yy))
            a1 = jnp.where(first, swap(xx), yy)
            (fslots if di < 2 and h == 0 else bslots).extend([a0, a1, xy])
    for i in range(0, 18, 2):
        gbs[8 * i : 8 * i + 16, :] = jnp.concatenate([bslots[i], bslots[i + 1]], axis=0).astype(BF16)
    for i in range(6):
        gfs[8 * i : 8 * i + 8, :] = fslots[i]

    @pl.loop(0, NCH)
    def _(c):
        at = pl.multiple_of(c * CH, CH)
        wide = ub[:, pl.ds(at, CH + 2 * PAD)]
        right = pltpu.roll(wide, CH + 2 * PAD - 1, 1)[:, PAD : PAD + CH]
        left = pltpu.roll(wide, 1, 1)[:, PAD : PAD + CH]
        x = wide[:, PAD : PAD + CH]
        v = jnp.concatenate(
            [0.5 * (right[0:8] - left[0:8]), x[8:16], 0.5 * (x[16:24] - left[16:24]), x[24:32]], axis=0
        )
        hi = v.astype(BF16)
        lhs[0:32, pl.ds(at, CH)] = hi
        lhs[32:64, pl.ds(at, CH)] = (v - hi.astype(F32)).astype(BF16)

    bb = jnp.dot(lhs[...], cd[...], preferred_element_type=F32)
    bb = bb[0:32] + bb[32:64]
    gfs[48:56, :] = jnp.where(first, bb[16:24], bb[24:32])
    gfs[56:64, :] = jnp.where(first, bb[0:8], bb[8:16])

    def fold(a, b):
        sub = lax.broadcasted_iota(jnp.int32, (8, 128), 0)
        ra = jnp.sum(a, axis=0, keepdims=True)
        rb = jnp.sum(b, axis=0, keepdims=True)
        return jnp.where(sub == 0, ra, jnp.where(sub == 1, rb, 0.0))

    gfs[64:72, :] = fold(sums[0], sums[1])

    def gf_copy(to, slot):
        return remote(gfs, gf.at[slot], s_gf.at[to], r_gf.at[slot], k, to)

    def gb_copy(to, slot):
        return remote(gbs, gb.at[slot], s_gb.at[to], r_gb.at[slot], k, to)

    @pl.loop(1, NQ)
    def _(d):
        to = lax.rem(s + d, NQ)
        gf_copy(to, s).start()
        gb_copy(to, s).start()

    gf[s] = gfs[...]
    gb[s] = gbs[...]

    @pl.when(has_next)
    def _():
        mid_prev.wait_recv()
        bot_prev.wait_recv()

    j32[7:8, PAD : PAD + COLS] = jmid[...]
    j32[8 + HALF : 9 + HALF, PAD : PAD + COLS] = jbot[...]

    def arrive(c):
        @pl.when(has_prev)
        def _():
            f_copy(c).wait_recv()

        @pl.when(has_next)
        def _():
            j_copy(c).wait_recv()

        at = pl.multiple_of(c * CH, CH)
        j32[8 : 8 + HALF, pl.ds(at + PAD, CH)] = jb[:, pl.ds(at, CH)].astype(F32)

    def tally(i, d, x):
        a = jnp.zeros((8, CH), F32)
        b = jnp.zeros((8, CH), F32)
        for t in range(0, d.shape[0], 8):
            a = a + d[t : t + 8]
            b = b + d[t : t + 8] * x[t : t + 8]
        dsums[i] = dsums[i] + a[:, :128] + a[:, 128:]
        dsums[i + 1] = dsums[i + 1] + b[:, :128] + b[:, 128:]

    def contract(at, rows):
        v = jnp.concatenate([jnp.dot(sp[...], qd[i], preferred_element_type=F32) for i in range(2)], axis=0)
        v = jnp.concatenate(
            [v[0:8] + v[8:16], v[16:24] + v[24:32], v[32:40] + v[40:48], v[48:56] + v[56:64]], axis=0
        )
        hi = v.astype(BF16)
        lo = (v - hi.astype(F32)).astype(BF16)
        b = jnp.dot(jnp.concatenate([hi, lo], axis=0), cd[pl.ds(at, CH), :], preferred_element_type=F32)
        return b[0:32] + b[32:64]

    @pl.when(k == 0)
    def _():
        for d in anc_copies:
            d.wait()
        qd[...] = jnp.zeros_like(qd)

        @pl.loop(0, NCH)
        def _(c):
            at = pl.multiple_of(c * CH, CH)
            for r in range(0, HALF, RB):
                x = i32[8 + HALF + r : 8 + HALF + r + RB, pl.ds(at + PAD, CH)]
                d = ab[r : r + RB, pl.ds(at, CH)].astype(F32) - x
                qd[0, HALF + r : HALF + r + RB, :] = (d * lxb[HALF + r : HALF + r + RB, pl.ds(at, CH)]).astype(BF16)
                qd[1, HALF + r : HALF + r + RB, :] = (d * lyb[HALF + r : HALF + r + RB, pl.ds(at, CH)]).astype(BF16)
                tally(0, d, x)
            b = contract(at, 0)
            bdacc[0:8] = bdacc[0:8] + b[8:16]
            bdacc[16:24] = bdacc[16:24] + b[24:32]

    arrive(0)

    @pl.loop(0, NCH)
    def _(c):
        at = pl.multiple_of(c * CH, CH)

        @pl.when(c < NCH - 1)
        def _():
            arrive(c + 1)

        for r in range(0, HALF, RB):
            x = i32[8 + r : 8 + r + RB, pl.ds(at + PAD, CH)]
            d = fb[r : r + RB, pl.ds(at, CH)].astype(F32) - x
            qd[0, r : r + RB, :] = (d * lxb[r : r + RB, pl.ds(at, CH)]).astype(BF16)
            qd[1, r : r + RB, :] = (d * lyb[r : r + RB, pl.ds(at, CH)]).astype(BF16)
            tally(0, d, x)
            mid = j32[8 + r : 8 + r + RB, pl.ds(at, CH + 2 * PAD)]
            x = mid[:, PAD : PAD + CH]
            right = pltpu.roll(mid, CH + 2 * PAD - 1, 1)[:, PAD : PAD + CH]
            left = pltpu.roll(mid, 1, 1)[:, PAD : PAD + CH]
            tall = j32[r : r + RB + 16, pl.ds(at + PAD, CH)]
            below = pltpu.roll(tall, RB + 15, 0)[8 : 8 + RB]
            above = pltpu.roll(tall, 1, 0)[8 : 8 + RB]
            d = i32[8 + HALF + r : 8 + HALF + r + RB, pl.ds(at + PAD, CH)] - x
            qd[0, HALF + r : HALF + r + RB, :] = (d * (right - left)).astype(BF16)
            qd[1, HALF + r : HALF + r + RB, :] = (d * (below - above)).astype(BF16)
            tally(2, d, x)
        bdacc[...] = bdacc[...] + contract(at, 0)

    bds[0:8, :] = 0.5 * jnp.where(first, bdacc[0:8], bdacc[16:24])
    bhs[0:8, :] = 0.5 * jnp.where(first, bdacc[8:16], bdacc[24:32])
    bds[8:16, :] = fold(dsums[0], dsums[1])
    bhs[8:16, :] = fold(dsums[2], dsums[3])

    def bo_copy(to, slot):
        return remote(bds, bdo.at[slot], s_bo.at[to], r_bo.at[slot], k, to)

    def bh_copy(to, slot):
        return remote(bhs, bdh.at[slot], s_bh.at[to], r_bh.at[slot], jnp.minimum(k + 1, NC - 1), to)

    @pl.loop(0, NQ)
    def _(d):
        to = lax.rem(s + d, NQ)

        @pl.when(has_next)
        def _():
            bh_copy(to, s).start()

        @pl.when(d > 0)
        def _():
            bo_copy(to, s).start()

    bdo[s] = bds[...]

    @pl.loop(1, NQ)
    def _(d):
        p = lax.rem(s + d, NQ)
        gf_copy(p, p).wait_recv()
        gb_copy(p, p).wait_recv()

    row = lax.broadcasted_iota(jnp.int32, (GRID, 128), 0)
    wide_first = lax.broadcasted_iota(jnp.int32, (GRID, 128), 1) < GRID

    def merge(parts):
        even = jnp.concatenate(parts[0::2], axis=0)
        odd = jnp.concatenate(parts[1::2], axis=0)
        even = jnp.where(row < GRID - 2, pltpu.roll(even, GRID - 2, 0), 0.0)
        odd = jnp.where(row >= 2, pltpu.roll(odd, 2, 0), 0.0)
        return even + odd

    def place(di, h, which, v):
        if di:
            v = jnp.where(row < GRID - di, v, 0.0)
        if which < 2:
            ga[4 * di + 2 * h + which] = v
        else:
            o = swap(v)
            gx[4 * di + 2 * h] = jnp.where(wide_first, v, o)
            gx[4 * di + 2 * h + 1] = jnp.where(wide_first, o, v)

    fi = 0
    bi = 0
    for di in range(4):
        for h in range(2):
            for which in range(3):
                if di < 2 and h == 0:
                    v = merge([gf[p, 8 * fi : 8 * fi + 8, :] for p in range(NQ)])
                    fi += 1
                else:
                    o = 8 * (bi % 2)
                    b0 = 16 * (bi // 2)
                    v = merge([gb[p, b0 : b0 + 16, :].astype(F32)[o : o + 8] for p in range(NQ)])
                    bi += 1
                place(di, h, which, v)
    b_i = merge([gf[p, 48:56, :] for p in range(NQ)])
    b_1 = merge([gf[p, 56:64, :] for p in range(NQ)])

    def total(v):
        return jnp.sum(v, axis=(0, 1), keepdims=True)

    tot = gf[0, 64:72, :]
    for p in range(1, NQ):
        tot = tot + gf[p, 64:72, :]
    sum_i = total(tot[0:1])
    sum_ii = total(tot[1:2])

    @pl.loop(0, NQ)
    def _(p):
        @pl.when(p != s)
        def _():
            bo_copy(p, p).wait_recv()

        @pl.when(has_prev)
        def _():
            bh_copy(p, p).wait_recv()

    b_f = b_i + merge([bdo[p, 0:8, :] + bdh[p, 0:8, :] for p in range(NQ)])
    tot = bdo[0, 8:16, :] + bdh[0, 8:16, :]
    for p in range(1, NQ):
        tot = tot + bdo[p, 8:16, :] + bdh[p, 8:16, :]
    sum_f = sum_i + total(tot[0:1])
    sum_fi = sum_ii + total(tot[1:2])
    mean_f = sum_f * (1.0 / PIXELS)

    def apply_gram(c):
        cl = [c] + [pltpu.roll(c, 128 - d, 1) for d in range(1, 4)]
        cs = swap(c)
        csl = [cs] + [pltpu.roll(cs, 128 - d, 1) for d in range(1, 4)]
        out = None
        lacc = [None] * 4

        def add(a, b):
            return b if a is None else a + b

        for di in range(4):
            racc = None
            for dj in range(4):
                a = ga[4 * di + dj]
                x = gx[4 * di + dj]
                up = (lambda v: v) if di == 0 else (lambda v: pltpu.roll(v, GRID - di, 0))
                out = add(out, a * up(cl[dj]) + x * up(csl[dj]))
                if dj:
                    lacc[dj] = add(lacc[dj], a * up(c) + x * up(cs))
                if di:
                    racc = add(racc, a * cl[dj] + x * csl[dj])
                if di and dj:
                    racc = racc + pltpu.roll(a * c + x * cs, dj, 1)
            if di:
                out = out + pltpu.roll(racc, di, 0)
        for dj in range(1, 4):
            out = out + pltpu.roll(lacc[dj], dj, 1)
        return out

    def direction(c):
        if c is None:
            mean_w = sum_i * (1.0 / PIXELS)
            sq = sum_ii
            cross = sum_fi
            b_w = b_i
        else:
            h = apply_gram(c)
            mean_w = (sum_i + total(c * b_1)) * (1.0 / PIXELS)
            sq = sum_ii + total(c * (2.0 * b_i + h))
            cross = sum_fi + total(c * b_f)
            b_w = b_i + h
        var = sq - PIXELS * mean_w * mean_w
        cov = cross - PIXELS * mean_f * mean_w
        den = jnp.sqrt(var + EPS)
        ratio = cov / den / (var + EPS)
        grad = PIXELS * ((b_f - mean_f * b_1) / den - ratio * (b_w - mean_w * b_1))
        mag = total(grad * grad) * (1.0 / (GRID * 2 * GRID))
        return grad / jnp.sqrt(mag + EPS)

    rate = 1.0 / ITERATIONS

    def cp_copy(i):
        return remote(csend.at[i], cprev.at[i], s_cp.at[i], r_cp.at[i], jnp.minimum(k + 1, NC - 1), s)

    def cn_copy(i):
        return remote(csend.at[i], cnext.at[i], s_cn.at[i], r_cn.at[i], jnp.maximum(k - 1, 0), s)

    def exchange(i, c):
        csend[i] = c

        @pl.when(has_next)
        def _():
            cp_copy(i).start()

        @pl.when(has_prev)
        def _():
            cn_copy(i).start()

    def receive(i):
        @pl.when(has_prev)
        def _():
            cp_copy(i).wait_recv()

        @pl.when(has_next)
        def _():
            cn_copy(i).wait_recv()

    c = rate * direction(None)
    exchange(0, c)
    for i in range(1, ITERATIONS - 1):
        step = c + rate * direction(c)
        receive(i - 1)
        c = step + SMOOTHING * (cprev[i - 1] - 2.0 * c + cnext[i - 1])
        exchange(i, c)
    step = c + rate * direction(c)

    base = pl.multiple_of(lax.div(4 * s + 6, 8) * 8, 8)
    even = lax.rem(s, 2) == 0

    def window(v):
        cpad[8 : 8 + GRID] = v
        w = cpad[pl.ds(base, 16), :]
        return jnp.where(even, w[6:14], w[2:10])

    cw = window(c)
    mine = window(step) - jnp.where(k == 0, SMOOTHING, 0.0) * cw
    ew_s[...] = mine

    def ew_copy(to, slot):
        return remote(ew_s, ew.at[slot], s_ew.at[to], r_ew.at[slot], to, s)

    for kk in range(1, NC):
        @pl.when(kk > k)
        def _():
            ew_copy(kk, k).start()

    receive(ITERATIONS - 2)
    nxt = window(cnext[ITERATIONS - 2])
    own = mine + SMOOTHING * (nxt - cw)

    for kk in range(NC - 1):
        @pl.when(kk < k)
        def _():
            ew_copy(kk, kk).wait_recv()

    t = ew[0]
    for kk in range(1, NC - 1):
        t = t + ew[kk]
    t = t + own
    tw_s[...] = t

    def tw_copy(to, slot):
        return remote(tw_s, tw.at[slot], s_tw.at[to], r_tw.at[slot], k, to)

    @pl.loop(1, NQ)
    def _(d):
        tw_copy(lax.rem(s + d, NQ), s).start()

    tw[s] = t

    hi = t.astype(BF16)
    rest = t - hi.astype(F32)
    mid = rest.astype(BF16)
    low = (rest - mid.astype(F32)).astype(BF16)
    stack = jnp.concatenate(
        [v.astype(F32) for v in (hi, mid, low, hi, mid, hi)] + [jnp.zeros((80, 128), F32)], axis=0
    ).astype(BF16)
    mixed = jnp.dot(mx[...], stack, preferred_element_type=F32).astype(BF16).astype(F32) * 0.5
    big_first = lax.broadcasted_iota(jnp.int32, (ROWS, 128), 1) < GRID
    mixed_x = jnp.where(big_first, mixed, 0.0).astype(BF16)
    mixed_y = jnp.where(big_first, 0.0, mixed).astype(BF16)
    dims = (((1,), (1,)), ((), ()))

    @pl.loop(0, NCH)
    def _(c):
        at = pl.multiple_of(c * CH, CH)
        table = cd[pl.ds(at, CH), :]
        sx = lax.dot_general(mixed_x, table, dims, preferred_element_type=F32)
        sy = lax.dot_general(mixed_y, table, dims, preferred_element_type=F32)
        v = (
            i32[8 : 8 + ROWS, pl.ds(at + PAD, CH)]
            + sx * lxb[:, pl.ds(at, CH)]
            + sy * lyb[:, pl.ds(at, CH)]
        )
        reg[0, :, pl.ds(at, CH)] = v.astype(BF16)

    @pl.loop(1, NQ)
    def _(d):
        p = lax.rem(s + d, NQ)
        tw_copy(p, p).wait_recv()

    for m in range(8):
        acc[0, 8 * m : 8 * m + 8, :] = jnp.concatenate([tw[2 * m, 2:6, :], tw[2 * m + 1, 2:6, :]], axis=0)

    @pl.when(s > 0)
    def _():
        up_top.wait_send()

    @pl.when(s < NQ - 1)
    def _():
        down_bot.wait_send()

    @pl.when(has_prev)
    def _():
        mid_prev.wait_send()
        bot_prev.wait_send()

    @pl.loop(0, NCH)
    def _(c):
        @pl.when(has_next)
        def _():
            f_copy(c).wait_send()

        @pl.when(has_prev)
        def _():
            j_copy(c).wait_send()

    @pl.loop(0, NQ)
    def _(d):
        to = lax.rem(s + d, NQ)

        @pl.when(has_next)
        def _():
            bh_copy(to, s).wait_send()

        @pl.when(d > 0)
        def _():
            gf_copy(to, s).wait_send()
            gb_copy(to, s).wait_send()
            bo_copy(to, s).wait_send()
            tw_copy(to, s).wait_send()

    for i in range(ITERATIONS - 1):
        @pl.when(has_next)
        def _():
            cp_copy(i).wait_send()

        @pl.when(has_prev)
        def _():
            cn_copy(i).wait_send()

    for kk in range(1, NC):
        @pl.when(kk > k)
        def _():
            ew_copy(kk, k).wait_send()


def solution(mesh):
    c, rows, split, mix = tables()

    def body(sections, anchor):
        v = pltpu.VMEM
        dma = pltpu.SemaphoreType.DMA
        row = v((1, COLS), F32)
        win = v((NQ, 16, 128), F32)
        scratch = [
            v((ROWS, COLS), BF16), v((HALF, COLS), BF16), v((HALF, COLS), BF16), v((HALF, COLS), BF16),
            v((ROWS + 16, COLS + 2 * PAD), F32), v((HALF + 16, COLS + 2 * PAD), F32),
            v((ROWS, COLS), F32), v((ROWS, COLS), F32),
            v((COLS, 128), BF16), v((COLS, 256), BF16),
            v((3, 80, ROWS), BF16), v((32, ROWS), BF16), v((ROWS, 128), BF16),
            v((5, ROWS, CH), BF16), v((2, ROWS, CH), BF16), v((96, COLS), BF16),
            v((32, COLS + 2 * PAD), F32), v((64, COLS), BF16), v((32, 128), F32),
            v((2, 8, 128), F32), v((4, 8, 128), F32),
            row, row, row, row, row, row, row,
            v((72, 128), F32), v((144, 128), BF16), v((NQ, 72, 128), F32), v((NQ, 144, 128), BF16),
            v((16, GRID, 128), F32), v((16, GRID, 128), F32),
            v((16, 128), F32), v((16, 128), F32), win, win,
            v((GRID + 16, 128), F32), v((3, GRID, 128), F32), v((3, GRID, 128), F32), v((3, GRID, 128), F32),
            v((8, 128), F32), v((NC - 1, 8, 128), F32), v((8, 128), F32), v((NQ, 8, 128), F32),
            dma((4,)), dma((4,)), dma((2,)),
            dma((NCH,)), dma((NCH,)), dma((NCH,)), dma((NCH,)), dma((4,)), dma((4,)),
            dma((NQ,)), dma((NQ,)), dma((NQ,)), dma((NQ,)),
            dma((NQ,)), dma((NQ,)), dma((NQ,)), dma((NQ,)),
            dma((3,)), dma((3,)), dma((3,)), dma((3,)), dma((NC,)), dma((NC,)), dma((NQ,)), dma((NQ,)),
        ]
        anywhere = pl.BlockSpec(memory_space=pl.ANY)
        inside = pl.BlockSpec(memory_space=pltpu.VMEM)
        return pl.pallas_call(
            kernel,
            out_shape=(
                jax.ShapeDtypeStruct((1, ROWS, COLS), BF16),
                jax.ShapeDtypeStruct((1, GRID, 2 * GRID), F32),
            ),
            in_specs=[anywhere] * 6,
            out_specs=(inside, inside),
            scratch_shapes=scratch,
            compiler_params=pltpu.CompilerParams(
                collective_id=0, has_side_effects=True, vmem_limit_bytes=60 * 1024 * 1024
            ),
        )(
            sections, anchor,
            jnp.asarray(c, BF16), jnp.asarray(rows, BF16), jnp.asarray(split, BF16), jnp.asarray(mix, BF16),
        )

    return jax.shard_map(
        body, mesh=mesh,
        in_specs=(P("chain", "quad", None), P("quad", None)),
        out_specs=(P("chain", "quad", None), P("chain", None, None)),
        check_vma=False,
    )
```

profile of v0, /device:TPU:6, one launch (start us, length us, event | category | flops | bytes accessed | tf_op | source)
XLA Modules:
  0.0 65.2 jit_solution(14039175401312013431)
XLA Ops:
  0.6 60.8 %shard_map.77 = (bf16[1,256,4096]{2,1,0:T(8,128)(2,1)}, f32[1,64,128]{2,1,0:T(8,128)}) custom-call(bf16[1,256,4096]{2,1,0:T(8,128)(2,1)} %sec.1, bf16[256,4096]{1,0:T(8,128)(2,1)} %anc.1, bf16[4096,128]{1,0:T(8,128)(2,1)} %constant.8.clone.cd_in, bf16[3,80,256]{2,1,0:T(8,128)(2,1)} %constant.9.clone.rt_in, bf16[32,256]{1,0:T(8,128)(2,1)} %constant.10.clone.sp_in, ...), custom_call_target="tpu_custom_call" | custom-call | tf_op jit(solution)/shard_map/pallas_call | solution.py:815
  61.5 0.0 copy-start
  61.5 3.1 %copy.10 = bf16[1,256,4096]{2,1,0:T(8,128)(2,1)} copy(bf16[1,256,4096]{2,1,0:T(8,128)(2,1)} %get-tuple-element.4) | data formatting | bytes 4194304
  64.6 0.0 copy-done
  64.6 0.6 copy.11
Async XLA Ops:
  61.5 3.1 %copy-start = (f32[1,64,128]{2,1,0:T(8,128)S(1)}, f32[1,64,128]{2,1,0:T(8,128)}, u32[]{:S(2)}) copy-start(f32[1,64,128]{2,1,0:T(8,128)} %get-tuple-element.5) | copy-start | bytes 98308
where the time goes:
time: 65.4 us; the launch traced here: 65.2 us
  Pallas kernels  60.8 us (93%)
  local copies, waits for them, and re-layouts  3.75 us (6%)
    pallas_call x1, Pallas kernels, body(): pl.pallas_call(kernel, out_shape=(jax.ShapeDtypeStruct((1, ROWS, COLS), B...  60.8 us
    unnamed x4, local copies, waits for them, and re-layouts  3.75 us

commit v1 on v0

--- a/solution.py
+++ b/solution.py
@@ -19,6 +19,8 @@
 HALF = 128
 CH = 256
 NCH = COLS // CH
+CX = 512
+NX = COLS // CX
 PAD = 128
 NC = 8
 NQ = 16
@@ -76,12 +78,12 @@
     sec, anc, cd_in, rt_in, sp_in, mx_in,
     reg, acc,
     ib, fb, jb, ab, i32, j32, lxb, lyb, cd, w1, rt, sp, mx,
-    qb, qd, tg, ub, lhs, bdacc, sums, dsums,
+    qb, tb, gacc, qd, vb, ub, lhs, bdacc, sums, dsums,
     etop, ebot, emid, htop, hbot, jmid, jbot,
-    gfs, gbs, gf, gb, ga, gx, bds, bhs, bdo, bdh,
+    gs, gn, gp, gall, ga, gx, bms, bm, bds, bhs, bdo, bdh,
     cpad, csend, cprev, cnext, ew_s, ew, tw_s, tw,
-    sem_in, sem_c, sem_a,
-    s_f, r_f, s_j, r_j, s_h, r_h, s_gf, r_gf, s_gb, r_gb,
+    sem_in, sem_c, sem_a, rounds,
+    s_f, r_f, s_j, r_j, s_h, r_h, s_n, r_n, s_g, r_g, s_bm, r_bm,
     s_bo, r_bo, s_bh, r_bh, s_cp, r_cp, s_cn, r_cn, s_ew, r_ew, s_tw, r_tw,
 ):
     k = lax.axis_index("chain")
@@ -123,34 +125,25 @@
 
     barrier = pltpu.get_barrier_semaphore()
 
-    def hello(kk, qq):
-        pl.semaphore_signal(barrier, inc=1, device_id={"chain": kk, "quad": qq}, device_id_type=MESH)
-
-    @pl.loop(1, NQ)
-    def _(d):
-        hello(k, lax.rem(s + d, NQ))
-
-    @pl.loop(0, NQ)
-    def _(q):
-        @pl.when(has_next)
-        def _():
-            hello(k + 1, q)
-
-        @pl.when(has_prev)
-        def _():
-            hello(k - 1, q)
-
-    @pl.loop(0, NC)
-    def _(kk):
-        @pl.when((kk > k + 1) | (kk < k - 1))
-        def _():
-            hello(kk, s)
-
-    one = jnp.int32(1)
-    zero = jnp.int32(0)
-    nn = jnp.where(has_next, one, zero)
-    np_ = jnp.where(has_prev, one, zero)
-    partners = (NQ - 1) + NQ * nn + NQ * np_ + (NC - 1) - nn - np_
+    def hello(sem, step):
+        for sign in (1, -1):
+            kk = k + sign * step
+            pl.semaphore_signal(
+                sem, inc=1, device_id={"chain": k, "quad": lax.rem(s + sign * step + NQ, NQ)}, device_id_type=MESH
+            )
+
+            @pl.when((kk >= 0) & (kk < NC))
+            def _():
+                pl.semaphore_signal(sem, inc=1, device_id={"chain": kk, "quad": s}, device_id_type=MESH)
+
+    def heard(sem, step):
+        one = jnp.int32(1)
+        zero = jnp.int32(0)
+        pl.semaphore_wait(
+            sem, 2 + jnp.where(k >= step, one, zero) + jnp.where(k + step < NC, one, zero)
+        )
+
+    hello(barrier, 1)
 
     i32[:, :PAD] = jnp.zeros((ROWS + 16, PAD), F32)
     i32[:, PAD + COLS :] = jnp.zeros((ROWS + 16, PAD), F32)
@@ -159,6 +152,11 @@
     ub[:, :PAD] = jnp.zeros((32, PAD), F32)
     ub[:, PAD + COLS :] = jnp.zeros((32, PAD), F32)
     sums[...] = jnp.zeros_like(sums)
+    qb[1] = jnp.zeros((5, ROWS, CH), BF16)
+    tb[0] = jnp.zeros((96, CH), BF16)
+    gacc[...] = jnp.zeros_like(gacc)
+    qd[...] = jnp.zeros_like(qd)
+    vb[...] = jnp.zeros_like(vb)
     dsums[...] = jnp.zeros_like(dsums)
     bdacc[...] = jnp.zeros_like(bdacc)
     cpad[...] = jnp.zeros_like(cpad)
@@ -166,10 +164,12 @@
     @pl.when(s == 0)
     def _():
         htop[...] = jnp.zeros_like(htop)
+        gn[0] = jnp.zeros((96, 128), F32)
 
     @pl.when(s == NQ - 1)
     def _():
         hbot[...] = jnp.zeros_like(hbot)
+        gn[1] = jnp.zeros((96, 128), F32)
 
     @pl.when(k == 0)
     def _():
@@ -188,60 +188,60 @@
         def _():
             ew[j] = jnp.zeros((8, 128), F32)
 
+    heard(barrier, 1)
+    hello(rounds.at[0], 1)
+
+    def f_copy(c):
+        at = pl.multiple_of(c * CX, CX)
+        return remote(
+            sec.at[0, pl.ds(0, HALF), pl.ds(at, CX)], fb.at[:, pl.ds(at, CX)],
+            s_f, r_f.at[c], jnp.minimum(k + 1, NC - 1), s,
+        )
+
+    def j_copy(c):
+        at = pl.multiple_of(c * CX, CX)
+        return remote(
+            sec.at[0, pl.ds(HALF, HALF), pl.ds(at, CX)], jb.at[:, pl.ds(at, CX)],
+            s_j, r_j.at[c], jnp.maximum(k - 1, 0), s,
+        )
+
+    @pl.loop(0, NX)
+    def _(c):
+        @pl.when(has_next)
+        def _():
+            f_copy(c).start()
+
+        @pl.when(has_prev)
+        def _():
+            j_copy(c).start()
+
+    up_top = remote(etop, hbot, s_h.at[0], r_h.at[0], k, jnp.maximum(s - 1, 0))
+    down_bot = remote(ebot, htop, s_h.at[1], r_h.at[1], k, jnp.minimum(s + 1, NQ - 1))
+    mid_prev = remote(emid, jmid, s_h.at[2], r_h.at[2], jnp.maximum(k - 1, 0), s)
+    bot_prev = remote(hbot, jbot, s_h.at[3], r_h.at[3], jnp.maximum(k - 1, 0), s)
+
     for c in range(4):
         in_copy(c).wait()
+    etop[...] = ib[0:16, :].astype(F32)[0:1]
+    ebot[...] = ib[ROWS - 16 : ROWS, :].astype(F32)[15:16]
+    emid[...] = ib[HALF - 16 : HALF, :].astype(F32)[15:16]
+
+    @pl.when(s > 0)
+    def _():
+        up_top.start()
+
+    @pl.when(s < NQ - 1)
+    def _():
+        down_bot.start()
+
+    @pl.when(has_prev)
+    def _():
+        mid_prev.start()
 
     @pl.loop(0, NCH)
     def _(c):
         at = pl.multiple_of(c * CH, CH)
         i32[8 : 8 + ROWS, pl.ds(at + PAD, CH)] = ib[:, pl.ds(at, CH)].astype(F32)
-
-    etop[...] = i32[8:9, PAD : PAD + COLS]
-    ebot[...] = i32[7 + ROWS : 8 + ROWS, PAD : PAD + COLS]
-    emid[...] = i32[7 + HALF : 8 + HALF, PAD : PAD + COLS]
-
-    pl.semaphore_wait(barrier, partners)
-
-    up_top = remote(etop, hbot, s_h.at[0], r_h.at[0], k, jnp.maximum(s - 1, 0))
-    down_bot = remote(ebot, htop, s_h.at[1], r_h.at[1], k, jnp.minimum(s + 1, NQ - 1))
-    mid_prev = remote(emid, jmid, s_h.at[2], r_h.at[2], jnp.maximum(k - 1, 0), s)
-    bot_prev = remote(hbot, jbot, s_h.at[3], r_h.at[3], jnp.maximum(k - 1, 0), s)
-
-    @pl.when(s > 0)
-    def _():
-        up_top.start()
-
-    @pl.when(s < NQ - 1)
-    def _():
-        down_bot.start()
-
-    def f_copy(c):
-        at = pl.multiple_of(c * CH, CH)
-        return remote(
-            ib.at[pl.ds(0, HALF), pl.ds(at, CH)], fb.at[:, pl.ds(at, CH)],
-            s_f.at[c], r_f.at[c], jnp.minimum(k + 1, NC - 1), s,
-        )
-
-    def j_copy(c):
-        at = pl.multiple_of(c * CH, CH)
-        return remote(
-            ib.at[pl.ds(HALF, HALF), pl.ds(at, CH)], jb.at[:, pl.ds(at, CH)],
-            s_j.at[c], r_j.at[c], jnp.maximum(k - 1, 0), s,
-        )
-
-    @pl.when(has_prev)
-    def _():
-        mid_prev.start()
-
-    @pl.loop(0, NCH)
-    def _(c):
-        @pl.when(has_next)
-        def _():
-            f_copy(c).start()
-
-        @pl.when(has_prev)
-        def _():
-            j_copy(c).start()
 
     for d in consts:
         d.wait()
@@ -279,9 +279,7 @@
     variant = jnp.where(s == 0, 0, jnp.where(s == NQ - 1, 2, 1))
     RB = 32
 
-    @pl.loop(0, NCH)
-    def _(c):
-        at = pl.multiple_of(c * CH, CH)
+    def pixels(at, slot):
         s1 = jnp.zeros((8, CH), F32)
         s2 = jnp.zeros((8, CH), F32)
         for r in range(0, ROWS, RB):
@@ -296,49 +294,97 @@
             ly = below - above
             lxb[r : r + RB, pl.ds(at, CH)] = lx
             lyb[r : r + RB, pl.ds(at, CH)] = ly
-            qb[0, r : r + RB, :] = (lx * lx).astype(BF16)
-            qb[1, r : r + RB, :] = (lx * ly).astype(BF16)
-            qb[2, r : r + RB, :] = (ly * ly).astype(BF16)
-            qb[3, r : r + RB, :] = (x * right).astype(BF16)
-            qb[4, r : r + RB, :] = (x * below).astype(BF16)
+            qb[slot, 0, r : r + RB, :] = (lx * lx).astype(BF16)
+            qb[slot, 1, r : r + RB, :] = (lx * ly).astype(BF16)
+            qb[slot, 2, r : r + RB, :] = (ly * ly).astype(BF16)
+            qb[slot, 3, r : r + RB, :] = (x * right).astype(BF16)
+            qb[slot, 4, r : r + RB, :] = (x * below).astype(BF16)
             for t in range(0, RB, 8):
                 xt = x[t : t + 8]
                 s1 = s1 + xt
                 s2 = s2 + xt * xt
         sums[0] = sums[0] + s1[:, :128] + s1[:, 128:]
         sums[1] = sums[1] + s2[:, :128] + s2[:, 128:]
+
+    def rows_out(at, slot):
         for i in range(3):
-            tg[32 * i : 32 * i + 32, pl.ds(at, CH)] = jnp.dot(
-                rt[variant, 0:32, :], qb[i], preferred_element_type=F32
+            tb[slot, 32 * i : 32 * i + 32, :] = jnp.dot(
+                rt[variant, 0:32, :], qb[slot, i], preferred_element_type=F32
             ).astype(BF16)
         u = jnp.dot(rt[variant, 32:64, :], ib[:, pl.ds(at, CH)], preferred_element_type=F32)
-        z = jnp.dot(rt[variant, 32:48, :], qb[3], preferred_element_type=F32)
-        q = jnp.dot(rt[variant, 64:80, :], qb[4], preferred_element_type=F32)
+        z = jnp.dot(rt[variant, 32:48, :], qb[slot, 3], preferred_element_type=F32)
+        q = jnp.dot(rt[variant, 64:80, :], qb[slot, 4], preferred_element_type=F32)
         ub[0:8, pl.ds(at + PAD, CH)] = u[0:8] + u[8:16]
         ub[8:16, pl.ds(at + PAD, CH)] = u[16:24] + u[24:32]
         ub[16:24, pl.ds(at + PAD, CH)] = z[0:8] + z[8:16]
         ub[24:32, pl.ds(at + PAD, CH)] = q[0:8] + q[8:16]
 
-    g = jnp.dot(tg[...], w1[...], preferred_element_type=F32) * 0.25
+    def columns_out(at, slot):
+        gacc[...] = gacc[...] + jnp.dot(tb[slot], w1[pl.ds(at, CH), :], preferred_element_type=F32)
+
+    def spot(c):
+        return pl.multiple_of(jnp.maximum(c, 0) * CH, CH)
+
+    @pl.loop(0, NCH // 2)
+    def _(p):
+        @pl.when(p == 1)
+        def _():
+            heard(rounds.at[0], 1)
+            hello(rounds.at[1], 2)
+
+        @pl.when(p == 4)
+        def _():
+            heard(rounds.at[1], 2)
+            hello(rounds.at[2], 4)
+
+        @pl.when(p == 7)
+        def _():
+            heard(rounds.at[2], 4)
+            hello(rounds.at[3], 1)
+
+        for u in range(2):
+            c = 2 * p + u
+            columns_out(spot(c - 2), u)
+            pixels(spot(c), u)
+            rows_out(spot(c - 1), 1 - u)
+
+    columns_out(spot(NCH - 2), 0)
+    rows_out(spot(NCH - 1), 1)
+    columns_out(spot(NCH - 1), 1)
+
     first = lane < GRID
 
     def swap(v):
         return pltpu.roll(v, GRID, 1)
 
-    fslots = []
-    bslots = []
+    quarter = lax.broadcasted_iota(jnp.int32, (8, 128), 0)
+
+    def pack(a, b):
+        return jnp.where(quarter < 4, pltpu.roll(a, 6, 0), pltpu.roll(b, 2, 0))
+
+    slots = []
     for di in range(4):
         for h in range(2):
-            xx = g[8 * di : 8 * di + 8, 128 * h : 128 * h + 128]
-            xy = g[32 + 8 * di : 40 + 8 * di, 128 * h : 128 * h + 128]
-            yy = g[64 + 8 * di : 72 + 8 * di, 128 * h : 128 * h + 128]
-            a0 = jnp.where(first, xx, swap(yy))
-            a1 = jnp.where(first, swap(xx), yy)
-            (fslots if di < 2 and h == 0 else bslots).extend([a0, a1, xy])
-    for i in range(0, 18, 2):
-        gbs[8 * i : 8 * i + 16, :] = jnp.concatenate([bslots[i], bslots[i + 1]], axis=0).astype(BF16)
-    for i in range(6):
-        gfs[8 * i : 8 * i + 8, :] = fslots[i]
+            part = lambda q: 0.25 * gacc[32 * q + 8 * di : 32 * q + 8 * di + 8, 128 * h : 128 * h + 128]
+            xx, xy, yy = part(0), part(1), part(2)
+            slots.append(jnp.where(first, xx, swap(yy)))
+            slots.append(jnp.where(first, swap(xx), yy))
+            slots.append(xy)
+    for i in range(12):
+        a, b = slots[2 * i], slots[2 * i + 1]
+        gs[8 * i : 8 * i + 8, :] = pack(a, b)
+        gp[8 * i : 8 * i + 8, :] = pack(pltpu.roll(a, 4, 0), pltpu.roll(b, 4, 0))
+
+    to_next = remote(gp, gn.at[0], s_n.at[0], r_n.at[0], k, jnp.minimum(s + 1, NQ - 1))
+    to_prev = remote(gp, gn.at[1], s_n.at[1], r_n.at[1], k, jnp.maximum(s - 1, 0))
+
+    @pl.when(s < NQ - 1)
+    def _():
+        to_next.start()
+
+    @pl.when(s > 0)
+    def _():
+        to_prev.start()
 
     @pl.loop(0, NCH)
     def _(c):
@@ -356,31 +402,44 @@
 
     bb = jnp.dot(lhs[...], cd[...], preferred_element_type=F32)
     bb = bb[0:32] + bb[32:64]
-    gfs[48:56, :] = jnp.where(first, bb[16:24], bb[24:32])
-    gfs[56:64, :] = jnp.where(first, bb[0:8], bb[8:16])
+    bms[0:8, :] = jnp.where(first, bb[16:24], bb[24:32])
+    bms[8:16, :] = jnp.where(first, bb[0:8], bb[8:16])
 
     def fold(a, b):
-        sub = lax.broadcasted_iota(jnp.int32, (8, 128), 0)
         ra = jnp.sum(a, axis=0, keepdims=True)
         rb = jnp.sum(b, axis=0, keepdims=True)
-        return jnp.where(sub == 0, ra, jnp.where(sub == 1, rb, 0.0))
-
-    gfs[64:72, :] = fold(sums[0], sums[1])
-
-    def gf_copy(to, slot):
-        return remote(gfs, gf.at[slot], s_gf.at[to], r_gf.at[slot], k, to)
-
-    def gb_copy(to, slot):
-        return remote(gbs, gb.at[slot], s_gb.at[to], r_gb.at[slot], k, to)
+        return jnp.where(quarter == 0, ra, jnp.where(quarter == 1, rb, 0.0))
+
+    bms[16:24, :] = fold(sums[0], sums[1])
+    bm[s] = bms[...]
+
+    @pl.when(s > 0)
+    def _():
+        to_next.wait_recv()
+
+    @pl.when(s < NQ - 1)
+    def _():
+        to_prev.wait_recv()
+
+    for i in range(12):
+        b8 = slice(8 * i, 8 * i + 8)
+        g = gs[b8, :] + jnp.where((quarter == 0) | (quarter == 1) | (quarter == 4) | (quarter == 5), gn[0, b8, :], gn[1, b8, :])
+        gs[b8, :] = g
+        gall[s, b8, :] = g
+
+    def g_copy(to, slot):
+        return remote(gs, gall.at[slot], s_g, r_g, k, to)
+
+    def bm_copy(to, slot):
+        return remote(bms, bm.at[slot], s_bm, r_bm, k, to)
 
     @pl.loop(1, NQ)
     def _(d):
         to = lax.rem(s + d, NQ)
-        gf_copy(to, s).start()
-        gb_copy(to, s).start()
-
-    gf[s] = gfs[...]
-    gb[s] = gbs[...]
+        bm_copy(to, s).start()
+        g_copy(to, s).start()
+
+    heard(rounds.at[3], 1)
 
     @pl.when(has_next)
     def _():
@@ -389,18 +448,6 @@
 
     j32[7:8, PAD : PAD + COLS] = jmid[...]
     j32[8 + HALF : 9 + HALF, PAD : PAD + COLS] = jbot[...]
-
-    def arrive(c):
-        @pl.when(has_prev)
-        def _():
-            f_copy(c).wait_recv()
-
-        @pl.when(has_next)
-        def _():
-            j_copy(c).wait_recv()
-
-        at = pl.multiple_of(c * CH, CH)
-        j32[8 : 8 + HALF, pl.ds(at + PAD, CH)] = jb[:, pl.ds(at, CH)].astype(F32)
 
     def tally(i, d, x):
         a = jnp.zeros((8, CH), F32)
@@ -411,51 +458,38 @@
         dsums[i] = dsums[i] + a[:, :128] + a[:, 128:]
         dsums[i + 1] = dsums[i + 1] + b[:, :128] + b[:, 128:]
 
-    def contract(at, rows):
-        v = jnp.concatenate([jnp.dot(sp[...], qd[i], preferred_element_type=F32) for i in range(2)], axis=0)
+    def cross_rows(slot):
+        v = jnp.concatenate(
+            [jnp.dot(sp[...], qd[slot, i], preferred_element_type=F32) for i in range(2)], axis=0
+        )
         v = jnp.concatenate(
             [v[0:8] + v[8:16], v[16:24] + v[24:32], v[32:40] + v[40:48], v[48:56] + v[56:64]], axis=0
         )
         hi = v.astype(BF16)
-        lo = (v - hi.astype(F32)).astype(BF16)
-        b = jnp.dot(jnp.concatenate([hi, lo], axis=0), cd[pl.ds(at, CH), :], preferred_element_type=F32)
-        return b[0:32] + b[32:64]
-
-    @pl.when(k == 0)
-    def _():
-        for d in anc_copies:
-            d.wait()
-        qd[...] = jnp.zeros_like(qd)
-
-        @pl.loop(0, NCH)
-        def _(c):
-            at = pl.multiple_of(c * CH, CH)
-            for r in range(0, HALF, RB):
-                x = i32[8 + HALF + r : 8 + HALF + r + RB, pl.ds(at + PAD, CH)]
-                d = ab[r : r + RB, pl.ds(at, CH)].astype(F32) - x
-                qd[0, HALF + r : HALF + r + RB, :] = (d * lxb[HALF + r : HALF + r + RB, pl.ds(at, CH)]).astype(BF16)
-                qd[1, HALF + r : HALF + r + RB, :] = (d * lyb[HALF + r : HALF + r + RB, pl.ds(at, CH)]).astype(BF16)
-                tally(0, d, x)
-            b = contract(at, 0)
-            bdacc[0:8] = bdacc[0:8] + b[8:16]
-            bdacc[16:24] = bdacc[16:24] + b[24:32]
-
-    arrive(0)
-
-    @pl.loop(0, NCH)
-    def _(c):
-        at = pl.multiple_of(c * CH, CH)
-
-        @pl.when(c < NCH - 1)
-        def _():
-            arrive(c + 1)
-
+        vb[slot, 0:32, :] = hi
+        vb[slot, 32:64, :] = (v - hi.astype(F32)).astype(BF16)
+
+    def cross_columns(at, slot):
+        b = jnp.dot(vb[slot], cd[pl.ds(at, CH), :], preferred_element_type=F32)
+        bdacc[...] = bdacc[...] + b[0:32] + b[32:64]
+
+    def lower(at, slot):
+        for r in range(0, HALF, RB):
+            rr = HALF + r
+            x = i32[8 + rr : 8 + rr + RB, pl.ds(at + PAD, CH)]
+            d = ab[r : r + RB, pl.ds(at, CH)].astype(F32) - x
+            qd[slot, 0, rr : rr + RB, :] = (d * lxb[rr : rr + RB, pl.ds(at, CH)]).astype(BF16)
+            qd[slot, 1, rr : rr + RB, :] = (d * lyb[rr : rr + RB, pl.ds(at, CH)]).astype(BF16)
+            tally(0, d, x)
+
+    def both(at, slot):
         for r in range(0, HALF, RB):
             x = i32[8 + r : 8 + r + RB, pl.ds(at + PAD, CH)]
             d = fb[r : r + RB, pl.ds(at, CH)].astype(F32) - x
-            qd[0, r : r + RB, :] = (d * lxb[r : r + RB, pl.ds(at, CH)]).astype(BF16)
-            qd[1, r : r + RB, :] = (d * lyb[r : r + RB, pl.ds(at, CH)]).astype(BF16)
+            qd[slot, 0, r : r + RB, :] = (d * lxb[r : r + RB, pl.ds(at, CH)]).astype(BF16)
+            qd[slot, 1, r : r + RB, :] = (d * lyb[r : r + RB, pl.ds(at, CH)]).astype(BF16)
             tally(0, d, x)
+            rr = HALF + r
             mid = j32[8 + r : 8 + r + RB, pl.ds(at, CH + 2 * PAD)]
             x = mid[:, PAD : PAD + CH]
             right = pltpu.roll(mid, CH + 2 * PAD - 1, 1)[:, PAD : PAD + CH]
@@ -463,11 +497,55 @@
             tall = j32[r : r + RB + 16, pl.ds(at + PAD, CH)]
             below = pltpu.roll(tall, RB + 15, 0)[8 : 8 + RB]
             above = pltpu.roll(tall, 1, 0)[8 : 8 + RB]
-            d = i32[8 + HALF + r : 8 + HALF + r + RB, pl.ds(at + PAD, CH)] - x
-            qd[0, HALF + r : HALF + r + RB, :] = (d * (right - left)).astype(BF16)
-            qd[1, HALF + r : HALF + r + RB, :] = (d * (below - above)).astype(BF16)
+            d = i32[8 + rr : 8 + rr + RB, pl.ds(at + PAD, CH)] - x
+            qd[slot, 0, rr : rr + RB, :] = (d * (right - left)).astype(BF16)
+            qd[slot, 1, rr : rr + RB, :] = (d * (below - above)).astype(BF16)
             tally(2, d, x)
-        bdacc[...] = bdacc[...] + contract(at, 0)
+
+    def cross(work, ahead):
+        @pl.loop(0, NCH // 2)
+        def _(p):
+            for u in range(2):
+                c = 2 * p + u
+                if ahead is not None:
+                    ahead(c + 1)
+                cross_columns(spot(c - 2), u)
+                work(spot(c), u)
+                cross_rows(1 - u)
+
+        cross_columns(spot(NCH - 2), 0)
+        cross_rows(1)
+        cross_columns(spot(NCH - 1), 1)
+
+    @pl.when(k == 0)
+    def _():
+        for d in anc_copies:
+            d.wait()
+        cross(lower, None)
+        bdacc[0:8] = bdacc[8:16]
+        bdacc[16:24] = bdacc[24:32]
+        bdacc[8:16] = jnp.zeros((8, 128), F32)
+        bdacc[24:32] = jnp.zeros((8, 128), F32)
+        qd[1] = jnp.zeros((2, ROWS, CH), BF16)
+        vb[...] = jnp.zeros_like(vb)
+
+    def arrive(c):
+        whole = lax.rem(c, CX // CH) == 0
+        piece = lax.div(c, CX // CH)
+
+        @pl.when(has_prev & whole & (c < NCH))
+        def _():
+            f_copy(piece).wait_recv()
+
+        @pl.when(has_next & whole & (c < NCH))
+        def _():
+            j_copy(piece).wait_recv()
+
+        at = pl.multiple_of(jnp.minimum(c, NCH - 1) * CH, CH)
+        j32[8 : 8 + HALF, pl.ds(at + PAD, CH)] = jb[:, pl.ds(at, CH)].astype(F32)
+
+    arrive(jnp.int32(0))
+    cross(both, arrive)
 
     bds[0:8, :] = 0.5 * jnp.where(first, bdacc[0:8], bdacc[16:24])
     bhs[0:8, :] = 0.5 * jnp.where(first, bdacc[8:16], bdacc[24:32])
@@ -475,10 +553,10 @@
     bhs[8:16, :] = fold(dsums[2], dsums[3])
 
     def bo_copy(to, slot):
-        return remote(bds, bdo.at[slot], s_bo.at[to], r_bo.at[slot], k, to)
+        return remote(bds, bdo.at[slot], s_bo, r_bo, k, to)
 
     def bh_copy(to, slot):
-        return remote(bhs, bdh.at[slot], s_bh.at[to], r_bh.at[slot], jnp.minimum(k + 1, NC - 1), to)
+        return remote(bhs, bdh.at[slot], s_bh, r_bh, jnp.minimum(k + 1, NC - 1), to)
 
     @pl.loop(0, NQ)
     def _(d):
@@ -494,14 +572,13 @@
 
     bdo[s] = bds[...]
 
-    @pl.loop(1, NQ)
-    def _(d):
-        p = lax.rem(s + d, NQ)
-        gf_copy(p, p).wait_recv()
-        gb_copy(p, p).wait_recv()
+    def all_of(ref, n, ss, rs):
+        return remote(ref.at[pl.ds(0, n)], ref.at[pl.ds(0, n)], ss, rs, k, lax.rem(s + 1, NQ))
+
+    all_of(bm, NQ - 1, s_bm, r_bm).wait_recv()
+    all_of(gall, NQ - 1, s_g, r_g).wait_recv()
 
     row = lax.broadcasted_iota(jnp.int32, (GRID, 128), 0)
-    wide_first = lax.broadcasted_iota(jnp.int32, (GRID, 128), 1) < GRID
 
     def merge(parts):
         even = jnp.concatenate(parts[0::2], axis=0)
@@ -510,51 +587,43 @@
         odd = jnp.where(row >= 2, pltpu.roll(odd, 2, 0), 0.0)
         return even + odd
 
-    def place(di, h, which, v):
-        if di:
-            v = jnp.where(row < GRID - di, v, 0.0)
-        if which < 2:
-            ga[4 * di + 2 * h + which] = v
-        else:
-            o = swap(v)
-            gx[4 * di + 2 * h] = jnp.where(wide_first, v, o)
-            gx[4 * di + 2 * h + 1] = jnp.where(wide_first, o, v)
-
-    fi = 0
-    bi = 0
-    for di in range(4):
-        for h in range(2):
-            for which in range(3):
-                if di < 2 and h == 0:
-                    v = merge([gf[p, 8 * fi : 8 * fi + 8, :] for p in range(NQ)])
-                    fi += 1
+    for i in range(12):
+        for m in range(8):
+            a = gall[2 * m, 8 * i : 8 * i + 8, :]
+            b = gall[2 * m + 1, 8 * i : 8 * i + 8, :]
+            pair = (
+                jnp.where(quarter < 4, a, pltpu.roll(b, 4, 0)),
+                jnp.where(quarter < 4, pltpu.roll(a, 4, 0), b),
+            )
+            for j in range(2):
+                di, h, which = (2 * i + j) // 6, ((2 * i + j) // 3) % 2, (2 * i + j) % 3
+                v = pair[j]
+                if di and m == 7:
+                    v = jnp.where(quarter < 8 - di, v, 0.0)
+                m8 = slice(8 * m, 8 * m + 8)
+                if which < 2:
+                    ga[4 * di + 2 * h + which, m8, :] = v
                 else:
-                    o = 8 * (bi % 2)
-                    b0 = 16 * (bi // 2)
-                    v = merge([gb[p, b0 : b0 + 16, :].astype(F32)[o : o + 8] for p in range(NQ)])
-                    bi += 1
-                place(di, h, which, v)
-    b_i = merge([gf[p, 48:56, :] for p in range(NQ)])
-    b_1 = merge([gf[p, 56:64, :] for p in range(NQ)])
+                    o = swap(v)
+                    gx[4 * di + 2 * h, m8, :] = jnp.where(first, v, o)
+                    gx[4 * di + 2 * h + 1, m8, :] = jnp.where(first, o, v)
+    b_i = merge([bm[p, 0:8, :] for p in range(NQ)])
+    b_1 = merge([bm[p, 8:16, :] for p in range(NQ)])
 
     def total(v):
         return jnp.sum(v, axis=(0, 1), keepdims=True)
 
-    tot = gf[0, 64:72, :]
+    tot = bm[0, 16:24, :]
     for p in range(1, NQ):
-        tot = tot + gf[p, 64:72, :]
+        tot = tot + bm[p, 16:24, :]
     sum_i = total(tot[0:1])
     sum_ii = total(tot[1:2])
 
-    @pl.loop(0, NQ)
-    def _(p):
-        @pl.when(p != s)
-        def _():
-            bo_copy(p, p).wait_recv()
-
-        @pl.when(has_prev)
-        def _():
-            bh_copy(p, p).wait_recv()
+    all_of(bdo, NQ - 1, s_bo, r_bo).wait_recv()
+
+    @pl.when(has_prev)
+    def _():
+        all_of(bdh, NQ, s_bh, r_bh).wait_recv()
 
     b_f = b_i + merge([bdo[p, 0:8, :] + bdh[p, 0:8, :] for p in range(NQ)])
     tot = bdo[0, 8:16, :] + bdh[0, 8:16, :]
@@ -686,7 +755,7 @@
     tw_s[...] = t
 
     def tw_copy(to, slot):
-        return remote(tw_s, tw.at[slot], s_tw.at[to], r_tw.at[slot], k, to)
+        return remote(tw_s, tw.at[slot], s_tw, r_tw, k, to)
 
     @pl.loop(1, NQ)
     def _(d):
@@ -707,23 +776,21 @@
     mixed_y = jnp.where(big_first, 0.0, mixed).astype(BF16)
     dims = (((1,), (1,)), ((), ()))
 
-    @pl.loop(0, NCH)
-    def _(c):
-        at = pl.multiple_of(c * CH, CH)
-        table = cd[pl.ds(at, CH), :]
-        sx = lax.dot_general(mixed_x, table, dims, preferred_element_type=F32)
-        sy = lax.dot_general(mixed_y, table, dims, preferred_element_type=F32)
-        v = (
-            i32[8 : 8 + ROWS, pl.ds(at + PAD, CH)]
-            + sx * lxb[:, pl.ds(at, CH)]
-            + sy * lyb[:, pl.ds(at, CH)]
-        )
-        reg[0, :, pl.ds(at, CH)] = v.astype(BF16)
-
-    @pl.loop(1, NQ)
-    def _(d):
-        p = lax.rem(s + d, NQ)
-        tw_copy(p, p).wait_recv()
+    @pl.loop(0, NCH // 4)
+    def _(p):
+        for u in range(4):
+            at = pl.multiple_of((4 * p + u) * CH, CH)
+            table = cd[pl.ds(at, CH), :]
+            sx = lax.dot_general(mixed_x, table, dims, preferred_element_type=F32)
+            sy = lax.dot_general(mixed_y, table, dims, preferred_element_type=F32)
+            v = (
+                i32[8 : 8 + ROWS, pl.ds(at + PAD, CH)]
+                + sx * lxb[:, pl.ds(at, CH)]
+                + sy * lyb[:, pl.ds(at, CH)]
+            )
+            reg[0, :, pl.ds(at, CH)] = v.astype(BF16)
+
+    all_of(tw, NQ - 1, s_tw, r_tw).wait_recv()
 
     for m in range(8):
         acc[0, 8 * m : 8 * m + 8, :] = jnp.concatenate([tw[2 * m, 2:6, :], tw[2 * m + 1, 2:6, :]], axis=0)
@@ -741,30 +808,32 @@
         mid_prev.wait_send()
         bot_prev.wait_send()
 
-    @pl.loop(0, NCH)
-    def _(c):
-        @pl.when(has_next)
-        def _():
-            f_copy(c).wait_send()
-
-        @pl.when(has_prev)
-        def _():
-            j_copy(c).wait_send()
-
-    @pl.loop(0, NQ)
-    def _(d):
-        to = lax.rem(s + d, NQ)
-
-        @pl.when(has_next)
-        def _():
-            bh_copy(to, s).wait_send()
-
-        @pl.when(d > 0)
-        def _():
-            gf_copy(to, s).wait_send()
-            gb_copy(to, s).wait_send()
-            bo_copy(to, s).wait_send()
-            tw_copy(to, s).wait_send()
+    half = sec.at[0, pl.ds(0, HALF)]
+
+    @pl.when(has_next)
+    def _():
+        remote(half, fb, s_f, r_f.at[0], jnp.minimum(k + 1, NC - 1), s).wait_send()
+
+    @pl.when(has_prev)
+    def _():
+        remote(half, jb, s_j, r_j.at[0], jnp.maximum(k - 1, 0), s).wait_send()
+
+    @pl.when(s < NQ - 1)
+    def _():
+        to_next.wait_send()
+
+    @pl.when(s > 0)
+    def _():
+        to_prev.wait_send()
+
+    @pl.when(has_next)
+    def _():
+        all_of(bdh, NQ, s_bh, r_bh).wait_send()
+
+    all_of(gall, NQ - 1, s_g, r_g).wait_send()
+    all_of(bm, NQ - 1, s_bm, r_bm).wait_send()
+    all_of(bdo, NQ - 1, s_bo, r_bo).wait_send()
+    all_of(tw, NQ - 1, s_tw, r_tw).wait_send()
 
     for i in range(ITERATIONS - 1):
         @pl.when(has_next)
@@ -795,34 +864,34 @@
             v((ROWS, COLS), F32), v((ROWS, COLS), F32),
             v((COLS, 128), BF16), v((COLS, 256), BF16),
             v((3, 80, ROWS), BF16), v((32, ROWS), BF16), v((ROWS, 128), BF16),
-            v((5, ROWS, CH), BF16), v((2, ROWS, CH), BF16), v((96, COLS), BF16),
+            v((2, 5, ROWS, CH), BF16), v((2, 96, CH), BF16), v((96, CH), F32),
+            v((2, 2, ROWS, CH), BF16), v((2, 64, CH), BF16),
             v((32, COLS + 2 * PAD), F32), v((64, COLS), BF16), v((32, 128), F32),
             v((2, 8, 128), F32), v((4, 8, 128), F32),
             row, row, row, row, row, row, row,
-            v((72, 128), F32), v((144, 128), BF16), v((NQ, 72, 128), F32), v((NQ, 144, 128), BF16),
+            v((96, 128), F32), v((2, 96, 128), F32), v((96, 128), F32), v((NQ, 96, 128), F32),
             v((16, GRID, 128), F32), v((16, GRID, 128), F32),
-            v((16, 128), F32), v((16, 128), F32), win, win,
+            v((24, 128), F32), v((NQ, 24, 128), F32), v((16, 128), F32), v((16, 128), F32), win, win,
             v((GRID + 16, 128), F32), v((3, GRID, 128), F32), v((3, GRID, 128), F32), v((3, GRID, 128), F32),
             v((8, 128), F32), v((NC - 1, 8, 128), F32), v((8, 128), F32), v((NQ, 8, 128), F32),
-            dma((4,)), dma((4,)), dma((2,)),
-            dma((NCH,)), dma((NCH,)), dma((NCH,)), dma((NCH,)), dma((4,)), dma((4,)),
-            dma((NQ,)), dma((NQ,)), dma((NQ,)), dma((NQ,)),
-            dma((NQ,)), dma((NQ,)), dma((NQ,)), dma((NQ,)),
-            dma((3,)), dma((3,)), dma((3,)), dma((3,)), dma((NC,)), dma((NC,)), dma((NQ,)), dma((NQ,)),
+            dma((4,)), dma((4,)), dma((2,)), pltpu.SemaphoreType.REGULAR((4,)),
+            dma, dma((NX,)), dma, dma((NX,)), dma((4,)), dma((4,)), dma((2,)), dma((2,)),
+            dma, dma, dma, dma, dma, dma, dma, dma,
+            dma((3,)), dma((3,)), dma((3,)), dma((3,)), dma((NC,)), dma((NC,)), dma, dma,
         ]
         anywhere = pl.BlockSpec(memory_space=pl.ANY)
         inside = pl.BlockSpec(memory_space=pltpu.VMEM)
         return pl.pallas_call(
             kernel,
             out_shape=(
-                jax.ShapeDtypeStruct((1, ROWS, COLS), BF16),
-                jax.ShapeDtypeStruct((1, GRID, 2 * GRID), F32),
+                pltpu.VMEM((1, ROWS, COLS), BF16),
+                pltpu.VMEM((1, GRID, 2 * GRID), F32),
             ),
             in_specs=[anywhere] * 6,
             out_specs=(inside, inside),
             scratch_shapes=scratch,
             compiler_params=pltpu.CompilerParams(
-                collective_id=0, has_side_effects=True, vmem_limit_bytes=60 * 1024 * 1024
+                collective_id=0, has_side_effects=True, vmem_limit_bytes=64_900_000
             ),
         )(
             sections, anchor,

time: 65.4 us -> 52 us (0.80)
  Pallas kernels: 60.8 us -> 49.2 us
  local copies, waits for them, and re-layouts: 3.75 us -> 1.94 us
    pallas_call x1, Pallas kernels: 60.8 us -> 49.2 us  [body(): pl.pallas_call(kernel, out_shape=(pltpu.VMEM((1, ROWS, COLS), BF16), pltp...]
    unnamed x4 -> x2, local copies, waits for them, and re-layouts: 3.75 us -> 1.94 us
where the time goes in v1:
time: 52 us; the launch traced here: 51.8 us
  Pallas kernels  49.2 us (95%)
  local copies, waits for them, and re-layouts  1.94 us (4%)
  between operations  0.64 us (1%)
    pallas_call x1, Pallas kernels, body(): pl.pallas_call(kernel, out_shape=(pltpu.VMEM((1, ROWS, COLS), BF16), pltp...  49.2 us
    unnamed x2, local copies, waits for them, and re-layouts  1.94 us

profile of v1, /device:TPU:6, one launch (start us, length us, event | category | flops | bytes accessed | tf_op | source)
XLA Modules:
  0.0 51.8 jit_solution(13281967657969454683)
XLA Ops:
  0.6 49.2 %shard_map.77 = (bf16[1,256,4096]{2,1,0:T(8,128)(2,1)S(1)}, f32[1,64,128]{2,1,0:T(8,128)S(1)}) custom-call(bf16[1,256,4096]{2,1,0:T(8,128)(2,1)} %sec.1, bf16[256,4096]{1,0:T(8,128)(2,1)} %anc.1, bf16[4096,128]{1,0:T(8,128)(2,1)} %constant.8.clone.cd_in, bf16[3,80,256]{2,1,0:T(8,128)(2,1)} %constant.9.clone.rt_in, bf16[32,256]{1,0:T(8,128)(2,1)} %constant.10.clone.sp_in, ...), custom_call_target="tpu_custom_call" | custom-call | tf_op jit(solution)/shard_map/pallas_call | solution.py:884
  49.9 1.3 %copy.10 = bf16[1,256,4096]{2,1,0:T(8,128)(2,1)} copy(bf16[1,256,4096]{2,1,0:T(8,128)(2,1)S(1)} %get-tuple-element.2) | data formatting | bytes 4194304
  51.2 0.6 %copy.11 = f32[1,64,128]{2,1,0:T(8,128)} copy(f32[1,64,128]{2,1,0:T(8,128)S(1)} %get-tuple-element.3) | data formatting | bytes 65536

commit v2 on v1

--- a/solution.py
+++ b/solution.py
@@ -16,7 +16,8 @@
 
 ROWS = 256
 COLS = 4096
-HALF = 128
+UP = 160
+LOW = ROWS - UP
 CH = 256
 NCH = COLS // CH
 CX = 512
@@ -65,7 +66,7 @@
             e[:, -1] = 0.0
         slope = 0.5 * (e[:, :-2] - e[:, 2:])
         rows.append(np.concatenate([pairs.reshape(32, ROWS)] + hi_lo(r) + hi_lo(slope) + hi_lo(step), axis=0))
-    top = (np.arange(ROWS) < HALF).astype(f)[None]
+    top = (np.arange(ROWS) < UP).astype(f)[None]
     split = np.concatenate([h * top for h in hi_lo(r)] + [h * (1 - top) for h in hi_lo(r)], axis=0)
     hi = bf(r)
     mid = bf(r - hi)
@@ -78,13 +79,13 @@
     sec, anc, cd_in, rt_in, sp_in, mx_in,
     reg, acc,
     ib, fb, jb, ab, i32, j32, lxb, lyb, cd, w1, rt, sp, mx,
-    qb, tb, gacc, qd, vb, ub, lhs, bdacc, sums, dsums,
+    wb, qb, tb, gacc, qd, vb, ub, lhs, bdacc, sums, dsums,
     etop, ebot, emid, htop, hbot, jmid, jbot,
-    gs, gn, gp, gall, ga, gx, bms, bm, bds, bhs, bdo, bdh,
+    gs, gn, gp, gt, gfs, gbs, gf, gb, ga, gx, bms, bm, bds, bhs, baa, bdo, bdh,
     cpad, csend, cprev, cnext, ew_s, ew, tw_s, tw,
     sem_in, sem_c, sem_a, rounds,
     s_f, r_f, s_j, r_j, s_h, r_h, s_n, r_n, s_g, r_g, s_bm, r_bm,
-    s_bo, r_bo, s_bh, r_bh, s_cp, r_cp, s_cn, r_cn, s_ew, r_ew, s_tw, r_tw,
+    s_bo, r_bo, s_bh, r_bh, s_ba, s_cp, r_cp, s_cn, r_cn, s_ew, r_ew, s_tw, r_tw,
 ):
     k = lax.axis_index("chain")
     s = lax.axis_index("quad")
@@ -114,8 +115,8 @@
     for d in consts:
         d.start()
     anc_copies = [
-        pltpu.make_async_copy(anc.at[pl.ds(0, HALF)], fb, sem_a.at[0]),
-        pltpu.make_async_copy(anc.at[pl.ds(HALF, HALF)], ab, sem_a.at[1]),
+        pltpu.make_async_copy(anc.at[pl.ds(0, UP)], fb, sem_a.at[0]),
+        pltpu.make_async_copy(anc.at[pl.ds(UP, LOW)], ab, sem_a.at[1]),
     ]
 
     @pl.when(k == 0)
@@ -147,8 +148,8 @@
 
     i32[:, :PAD] = jnp.zeros((ROWS + 16, PAD), F32)
     i32[:, PAD + COLS :] = jnp.zeros((ROWS + 16, PAD), F32)
-    j32[:, :PAD] = jnp.zeros((HALF + 16, PAD), F32)
-    j32[:, PAD + COLS :] = jnp.zeros((HALF + 16, PAD), F32)
+    j32[:, :PAD] = jnp.zeros((LOW + 16, PAD), F32)
+    j32[:, PAD + COLS :] = jnp.zeros((LOW + 16, PAD), F32)
     ub[:, :PAD] = jnp.zeros((32, PAD), F32)
     ub[:, PAD + COLS :] = jnp.zeros((32, PAD), F32)
     sums[...] = jnp.zeros_like(sums)
@@ -173,7 +174,6 @@
 
     @pl.when(k == 0)
     def _():
-        bdh[...] = jnp.zeros_like(bdh)
         cprev[...] = jnp.zeros_like(cprev)
 
     @pl.when(k == NC - 1)
@@ -194,14 +194,14 @@
     def f_copy(c):
         at = pl.multiple_of(c * CX, CX)
         return remote(
-            sec.at[0, pl.ds(0, HALF), pl.ds(at, CX)], fb.at[:, pl.ds(at, CX)],
+            sec.at[0, pl.ds(0, UP), pl.ds(at, CX)], fb.at[:, pl.ds(at, CX)],
             s_f, r_f.at[c], jnp.minimum(k + 1, NC - 1), s,
         )
 
     def j_copy(c):
         at = pl.multiple_of(c * CX, CX)
         return remote(
-            sec.at[0, pl.ds(HALF, HALF), pl.ds(at, CX)], jb.at[:, pl.ds(at, CX)],
+            sec.at[0, pl.ds(UP, LOW), pl.ds(at, CX)], jb.at[:, pl.ds(at, CX)],
             s_j, r_j.at[c], jnp.maximum(k - 1, 0), s,
         )
 
@@ -224,7 +224,7 @@
         in_copy(c).wait()
     etop[...] = ib[0:16, :].astype(F32)[0:1]
     ebot[...] = ib[ROWS - 16 : ROWS, :].astype(F32)[15:16]
-    emid[...] = ib[HALF - 16 : HALF, :].astype(F32)[15:16]
+    emid[...] = ib[UP - 16 : UP, :].astype(F32)[15:16]
 
     @pl.when(s > 0)
     def _():
@@ -237,29 +237,53 @@
     @pl.when(has_prev)
     def _():
         mid_prev.start()
-
-    @pl.loop(0, NCH)
-    def _(c):
-        at = pl.multiple_of(c * CH, CH)
-        i32[8 : 8 + ROWS, pl.ds(at + PAD, CH)] = ib[:, pl.ds(at, CH)].astype(F32)
 
     for d in consts:
         d.wait()
     lane = lax.broadcasted_iota(jnp.int32, (8, 128), 1)
 
-    @pl.loop(0, NCH)
-    def _(c):
+    v = cd[pl.ds(CH, CH), :].astype(F32)
+    ln = lax.broadcasted_iota(jnp.int32, (CH, 128), 1)
+    knot = jnp.where(ln < GRID, ln, ln - GRID)
+    for h in range(2):
+        a = v if h == 0 else pltpu.roll(v, 128 - 2 * h, 1)
+        b = pltpu.roll(v, 127 - 2 * h, 1)
+        wb[:, h * 128 : (h + 1) * 128] = v * jnp.where(ln < GRID, a, b)
+
+    @pl.loop(0, NCH // 4)
+    def _(c4):
+      for c in [4 * c4 + u for u in range(4)]:
         at = pl.multiple_of(c * CH, CH)
-        v = cd[pl.ds(at, CH), :].astype(F32)
-        ln = lax.broadcasted_iota(jnp.int32, (CH, 128), 1)
-        j = jnp.where(ln < GRID, ln, ln - GRID)
         for h in range(2):
-            lo_d, hi_d = 2 * h, 2 * h + 1
-            a = v if lo_d == 0 else pltpu.roll(v, 128 - lo_d, 1)
-            b = pltpu.roll(v, 128 - hi_d, 1)
-            a = jnp.where(j < GRID - lo_d, a, 0.0)
-            b = jnp.where(j < GRID - hi_d, b, 0.0)
-            w1[pl.ds(at, CH), h * 128 : (h + 1) * 128] = (v * jnp.where(ln < GRID, a, b)).astype(BF16)
+            partner = knot + jnp.where(ln < GRID, 2 * h, 2 * h + 1)
+            near = (jnp.abs(2 * (knot - 4 * c) - 3) < 16) & (partner < GRID)
+            t = pltpu.roll(wb[:, h * 128 : (h + 1) * 128], lax.rem(4 * c + 124, 128), 1)
+            w1[pl.ds(at, CH), h * 128 : (h + 1) * 128] = jnp.where(near, t, 0.0).astype(BF16)
+
+    variant = jnp.where(s == 0, 0, jnp.where(s == NQ - 1, 2, 1))
+    RB = 32
+
+    def spot(c):
+        return pl.multiple_of(jnp.maximum(c, 0) * CH, CH)
+
+    @pl.loop(0, NCH // 2)
+    def _(p):
+        for c in [2 * p, 2 * p + 1]:
+            at = pl.multiple_of(c * CH, CH)
+            u = jnp.dot(rt[variant, 32:64, :], ib[:, pl.ds(at, CH)], preferred_element_type=F32)
+            ub[0:8, pl.ds(at + PAD, CH)] = u[0:8] + u[8:16]
+            ub[8:16, pl.ds(at + PAD, CH)] = u[16:24] + u[24:32]
+            s1 = jnp.zeros((8, CH), F32)
+            s2 = jnp.zeros((8, CH), F32)
+            for r in range(0, ROWS, RB):
+                x = ib[r : r + RB, pl.ds(at, CH)].astype(F32)
+                i32[8 + r : 8 + r + RB, pl.ds(at + PAD, CH)] = x
+                for t in range(0, RB, 8):
+                    xt = x[t : t + 8]
+                    s1 = s1 + xt
+                    s2 = s2 + xt * xt
+            sums[0] = sums[0] + s1[:, :128] + s1[:, 128:]
+            sums[1] = sums[1] + s2[:, :128] + s2[:, 128:]
 
     @pl.when(s < NQ - 1)
     def _():
@@ -276,81 +300,98 @@
     i32[7:8, PAD : PAD + COLS] = htop[...]
     i32[8 + ROWS : 9 + ROWS, PAD : PAD + COLS] = hbot[...]
 
-    variant = jnp.where(s == 0, 0, jnp.where(s == NQ - 1, 2, 1))
-    RB = 32
-
-    def pixels(at, slot):
-        s1 = jnp.zeros((8, CH), F32)
-        s2 = jnp.zeros((8, CH), F32)
+    heard(rounds.at[0], 1)
+    hello(rounds.at[1], 2)
+
+    def tally(i, d, x):
+        a = jnp.zeros((8, CH), F32)
+        b = jnp.zeros((8, CH), F32)
+        for t in range(0, d.shape[0], 8):
+            a = a + d[t : t + 8]
+            b = b + d[t : t + 8] * x[t : t + 8]
+        dsums[i] = dsums[i] + a[:, :128] + a[:, 128:]
+        dsums[i + 1] = dsums[i + 1] + b[:, :128] + b[:, 128:]
+
+    def pixels(at, slot, with_anchor):
         for r in range(0, ROWS, RB):
             mid = i32[8 + r : 8 + r + RB, pl.ds(at, CH + 2 * PAD)]
             x = mid[:, PAD : PAD + CH]
             right = pltpu.roll(mid, CH + 2 * PAD - 1, 1)[:, PAD : PAD + CH]
             left = pltpu.roll(mid, 1, 1)[:, PAD : PAD + CH]
+            lx = right - left
+            lxb[r : r + RB, pl.ds(at, CH)] = lx
             tall = i32[r : r + RB + 16, pl.ds(at + PAD, CH)]
             below = pltpu.roll(tall, RB + 15, 0)[8 : 8 + RB]
             above = pltpu.roll(tall, 1, 0)[8 : 8 + RB]
-            lx = right - left
             ly = below - above
-            lxb[r : r + RB, pl.ds(at, CH)] = lx
             lyb[r : r + RB, pl.ds(at, CH)] = ly
             qb[slot, 0, r : r + RB, :] = (lx * lx).astype(BF16)
+            qb[slot, 3, r : r + RB, :] = (x * right).astype(BF16)
             qb[slot, 1, r : r + RB, :] = (lx * ly).astype(BF16)
             qb[slot, 2, r : r + RB, :] = (ly * ly).astype(BF16)
-            qb[slot, 3, r : r + RB, :] = (x * right).astype(BF16)
             qb[slot, 4, r : r + RB, :] = (x * below).astype(BF16)
-            for t in range(0, RB, 8):
-                xt = x[t : t + 8]
-                s1 = s1 + xt
-                s2 = s2 + xt * xt
-        sums[0] = sums[0] + s1[:, :128] + s1[:, 128:]
-        sums[1] = sums[1] + s2[:, :128] + s2[:, 128:]
-
-    def rows_out(at, slot):
+            if with_anchor:
+                src, rr = (fb, r) if r < UP else (ab, r - UP)
+                d = src[rr : rr + RB, pl.ds(at, CH)].astype(F32) - x
+                qd[slot, 0, r : r + RB, :] = (d * lx).astype(BF16)
+                qd[slot, 1, r : r + RB, :] = (d * ly).astype(BF16)
+                tally(0, d, x)
+
+    def rows_out(at, slot, with_anchor):
         for i in range(3):
-            tb[slot, 32 * i : 32 * i + 32, :] = jnp.dot(
+            tb[slot, 32 * i : 32 + 32 * i, :] = jnp.dot(
                 rt[variant, 0:32, :], qb[slot, i], preferred_element_type=F32
             ).astype(BF16)
-        u = jnp.dot(rt[variant, 32:64, :], ib[:, pl.ds(at, CH)], preferred_element_type=F32)
         z = jnp.dot(rt[variant, 32:48, :], qb[slot, 3], preferred_element_type=F32)
+        ub[16:24, pl.ds(at + PAD, CH)] = z[0:8] + z[8:16]
         q = jnp.dot(rt[variant, 64:80, :], qb[slot, 4], preferred_element_type=F32)
-        ub[0:8, pl.ds(at + PAD, CH)] = u[0:8] + u[8:16]
-        ub[8:16, pl.ds(at + PAD, CH)] = u[16:24] + u[24:32]
-        ub[16:24, pl.ds(at + PAD, CH)] = z[0:8] + z[8:16]
         ub[24:32, pl.ds(at + PAD, CH)] = q[0:8] + q[8:16]
-
-    def columns_out(at, slot):
+        if with_anchor:
+            for i in range(2):
+                v = jnp.dot(rt[variant, 32:48, :], qd[slot, i], preferred_element_type=F32)
+                v = v[0:8] + v[8:16]
+                hi = v.astype(BF16).astype(F32)
+                vb[slot, 16 * i : 16 * i + 16, :] = jnp.concatenate([hi, v - hi], axis=0).astype(BF16)
+
+    def columns_out(at, slot, with_anchor):
         gacc[...] = gacc[...] + jnp.dot(tb[slot], w1[pl.ds(at, CH), :], preferred_element_type=F32)
-
-    def spot(c):
-        return pl.multiple_of(jnp.maximum(c, 0) * CH, CH)
-
-    @pl.loop(0, NCH // 2)
-    def _(p):
-        @pl.when(p == 1)
-        def _():
-            heard(rounds.at[0], 1)
-            hello(rounds.at[1], 2)
-
-        @pl.when(p == 4)
-        def _():
-            heard(rounds.at[1], 2)
-            hello(rounds.at[2], 4)
-
-        @pl.when(p == 7)
-        def _():
-            heard(rounds.at[2], 4)
-            hello(rounds.at[3], 1)
-
-        for u in range(2):
-            c = 2 * p + u
-            columns_out(spot(c - 2), u)
-            pixels(spot(c), u)
-            rows_out(spot(c - 1), 1 - u)
-
-    columns_out(spot(NCH - 2), 0)
-    rows_out(spot(NCH - 1), 1)
-    columns_out(spot(NCH - 1), 1)
+        if with_anchor:
+            b = jnp.dot(vb[slot, 0:32, :], cd[pl.ds(at, CH), :], preferred_element_type=F32)
+            bdacc[0:8] = bdacc[0:8] + b[0:8] + b[8:16]
+            bdacc[16:24] = bdacc[16:24] + b[16:24] + b[24:32]
+
+    def own_pass(with_anchor):
+        @pl.loop(0, NCH // 2)
+        def _(p):
+            @pl.when(p == 3)
+            def _():
+                heard(rounds.at[1], 2)
+                hello(rounds.at[2], 4)
+
+            @pl.when(p == 7)
+            def _():
+                heard(rounds.at[2], 4)
+                hello(rounds.at[3], 1)
+
+            for u in range(2):
+                c = 2 * p + u
+                columns_out(spot(c - 2), u, with_anchor)
+                pixels(spot(c), u, with_anchor)
+                rows_out(spot(c - 1), 1 - u, with_anchor)
+
+        columns_out(spot(NCH - 2), 0, with_anchor)
+        rows_out(spot(NCH - 1), 1, with_anchor)
+        columns_out(spot(NCH - 1), 1, with_anchor)
+
+    @pl.when(k > 0)
+    def _():
+        own_pass(False)
+
+    @pl.when(k == 0)
+    def _():
+        for d in anc_copies:
+            d.wait()
+        own_pass(True)
 
     first = lane < GRID
 
@@ -362,14 +403,15 @@
     def pack(a, b):
         return jnp.where(quarter < 4, pltpu.roll(a, 6, 0), pltpu.roll(b, 2, 0))
 
+    order = [(di, h) for di in range(2) for h in range(1)]
+    order = order + [(di, h) for di in range(4) for h in range(2) if (di, h) not in order]
     slots = []
-    for di in range(4):
-        for h in range(2):
-            part = lambda q: 0.25 * gacc[32 * q + 8 * di : 32 * q + 8 * di + 8, 128 * h : 128 * h + 128]
-            xx, xy, yy = part(0), part(1), part(2)
-            slots.append(jnp.where(first, xx, swap(yy)))
-            slots.append(jnp.where(first, swap(xx), yy))
-            slots.append(xy)
+    for di, h in order:
+        part = lambda q: 0.25 * gacc[32 * q + 8 * di : 32 * q + 8 * di + 8, 128 * h : 128 * h + 128]
+        xx, xy, yy = part(0), part(1), part(2)
+        slots.append(jnp.where(first, xx, swap(yy)))
+        slots.append(jnp.where(first, swap(xx), yy))
+        slots.append(xy)
     for i in range(12):
         a, b = slots[2 * i], slots[2 * i + 1]
         gs[8 * i : 8 * i + 8, :] = pack(a, b)
@@ -386,8 +428,9 @@
     def _():
         to_prev.start()
 
-    @pl.loop(0, NCH)
-    def _(c):
+    @pl.loop(0, NCH // 4)
+    def _(c4):
+      for c in [4 * c4 + u for u in range(4)]:
         at = pl.multiple_of(c * CH, CH)
         wide = ub[:, pl.ds(at, CH + 2 * PAD)]
         right = pltpu.roll(wide, CH + 2 * PAD - 1, 1)[:, PAD : PAD + CH]
@@ -413,33 +456,44 @@
     bms[16:24, :] = fold(sums[0], sums[1])
     bm[s] = bms[...]
 
-    @pl.when(s > 0)
-    def _():
-        to_next.wait_recv()
-
-    @pl.when(s < NQ - 1)
-    def _():
-        to_prev.wait_recv()
-
-    for i in range(12):
-        b8 = slice(8 * i, 8 * i + 8)
-        g = gs[b8, :] + jnp.where((quarter == 0) | (quarter == 1) | (quarter == 4) | (quarter == 5), gn[0, b8, :], gn[1, b8, :])
-        gs[b8, :] = g
-        gall[s, b8, :] = g
-
-    def g_copy(to, slot):
-        return remote(gs, gall.at[slot], s_g, r_g, k, to)
-
     def bm_copy(to, slot):
         return remote(bms, bm.at[slot], s_bm, r_bm, k, to)
 
     @pl.loop(1, NQ)
     def _(d):
-        to = lax.rem(s + d, NQ)
-        bm_copy(to, s).start()
-        g_copy(to, s).start()
+        bm_copy(lax.rem(s + d, NQ), s).start()
 
     heard(rounds.at[3], 1)
+
+    def gf_copy(to, slot):
+        return remote(gfs, gf.at[slot], s_g.at[0], r_g.at[0], k, to)
+
+    def gb_copy(to, slot):
+        return remote(gbs, gb.at[slot], s_g.at[1], r_g.at[1], k, to)
+
+    def spread_gram():
+        @pl.when(s > 0)
+        def _():
+            to_next.wait_recv()
+
+        @pl.when(s < NQ - 1)
+        def _():
+            to_prev.wait_recv()
+
+        lower_rows = (quarter == 0) | (quarter == 1) | (quarter == 4) | (quarter == 5)
+        for i in range(12):
+            b8 = slice(8 * i, 8 * i + 8)
+            gt[b8, :] = gs[b8, :] + jnp.where(lower_rows, gn[0, b8, :], gn[1, b8, :])
+        gfs[...] = gt[0:24, :]
+        gbs[0:64, :] = gt[24:88, :].astype(BF16)
+        gbs[64:80, :] = jnp.concatenate([gt[88:96, :], jnp.zeros((8, 128), F32)], axis=0).astype(BF16)
+        gf[s] = gfs[...]
+        gb[s] = gbs[...]
+
+        @pl.loop(1, NQ)
+        def _(d):
+            to = lax.rem(s + d, NQ)
+            gf_copy(to, s).start()
 
     @pl.when(has_next)
     def _():
@@ -447,16 +501,14 @@
         bot_prev.wait_recv()
 
     j32[7:8, PAD : PAD + COLS] = jmid[...]
-    j32[8 + HALF : 9 + HALF, PAD : PAD + COLS] = jbot[...]
-
-    def tally(i, d, x):
-        a = jnp.zeros((8, CH), F32)
-        b = jnp.zeros((8, CH), F32)
-        for t in range(0, d.shape[0], 8):
-            a = a + d[t : t + 8]
-            b = b + d[t : t + 8] * x[t : t + 8]
-        dsums[i] = dsums[i] + a[:, :128] + a[:, 128:]
-        dsums[i + 1] = dsums[i + 1] + b[:, :128] + b[:, 128:]
+    j32[8 + LOW : 9 + LOW, PAD : PAD + COLS] = jbot[...]
+
+    def tuck(ref, at, a, b):
+        ref[at : at + 1, :] = jnp.sum(a, axis=0, keepdims=True)
+        ref[at + 1 : at + 2, :] = jnp.sum(b, axis=0, keepdims=True)
+
+    def ba_copy(to, slot):
+        return remote(baa, bdh.at[slot], s_ba, r_bh, k, to)
 
     def cross_rows(slot):
         v = jnp.concatenate(
@@ -473,23 +525,15 @@
         b = jnp.dot(vb[slot], cd[pl.ds(at, CH), :], preferred_element_type=F32)
         bdacc[...] = bdacc[...] + b[0:32] + b[32:64]
 
-    def lower(at, slot):
-        for r in range(0, HALF, RB):
-            rr = HALF + r
-            x = i32[8 + rr : 8 + rr + RB, pl.ds(at + PAD, CH)]
-            d = ab[r : r + RB, pl.ds(at, CH)].astype(F32) - x
-            qd[slot, 0, rr : rr + RB, :] = (d * lxb[rr : rr + RB, pl.ds(at, CH)]).astype(BF16)
-            qd[slot, 1, rr : rr + RB, :] = (d * lyb[rr : rr + RB, pl.ds(at, CH)]).astype(BF16)
-            tally(0, d, x)
-
-    def both(at, slot):
-        for r in range(0, HALF, RB):
+    def both(at, slot, upper):
+        for r in range(0, UP if upper else 0, RB):
             x = i32[8 + r : 8 + r + RB, pl.ds(at + PAD, CH)]
             d = fb[r : r + RB, pl.ds(at, CH)].astype(F32) - x
             qd[slot, 0, r : r + RB, :] = (d * lxb[r : r + RB, pl.ds(at, CH)]).astype(BF16)
             qd[slot, 1, r : r + RB, :] = (d * lyb[r : r + RB, pl.ds(at, CH)]).astype(BF16)
             tally(0, d, x)
-            rr = HALF + r
+        for r in range(0, LOW, RB):
+            rr = UP + r
             mid = j32[8 + r : 8 + r + RB, pl.ds(at, CH + 2 * PAD)]
             x = mid[:, PAD : PAD + CH]
             right = pltpu.roll(mid, CH + 2 * PAD - 1, 1)[:, PAD : PAD + CH]
@@ -502,15 +546,18 @@
             qd[slot, 1, rr : rr + RB, :] = (d * (below - above)).astype(BF16)
             tally(2, d, x)
 
-    def cross(work, ahead):
+    def cross(upper):
         @pl.loop(0, NCH // 2)
         def _(p):
+            @pl.when(p == 2)
+            def _():
+                spread_gram()
+
+            arrive(p + 1)
             for u in range(2):
                 c = 2 * p + u
-                if ahead is not None:
-                    ahead(c + 1)
                 cross_columns(spot(c - 2), u)
-                work(spot(c), u)
+                both(spot(c), u, upper)
                 cross_rows(1 - u)
 
         cross_columns(spot(NCH - 2), 0)
@@ -519,38 +566,43 @@
 
     @pl.when(k == 0)
     def _():
-        for d in anc_copies:
-            d.wait()
-        cross(lower, None)
-        bdacc[0:8] = bdacc[8:16]
-        bdacc[16:24] = bdacc[24:32]
-        bdacc[8:16] = jnp.zeros((8, 128), F32)
-        bdacc[24:32] = jnp.zeros((8, 128), F32)
-        qd[1] = jnp.zeros((2, ROWS, CH), BF16)
+        baa[0:8, :] = 0.5 * jnp.where(first, bdacc[0:8], bdacc[16:24])
+        bdacc[...] = jnp.zeros_like(bdacc)
+        qd[...] = jnp.zeros_like(qd)
         vb[...] = jnp.zeros_like(vb)
 
-    def arrive(c):
-        whole = lax.rem(c, CX // CH) == 0
-        piece = lax.div(c, CX // CH)
-
-        @pl.when(has_prev & whole & (c < NCH))
+        @pl.loop(1, NQ)
+        def _(d):
+            ba_copy(lax.rem(s + d, NQ), s).start()
+
+        bdh[s] = baa[...]
+
+    def arrive(piece):
+        @pl.when(has_prev & (piece < NX))
         def _():
             f_copy(piece).wait_recv()
 
-        @pl.when(has_next & whole & (c < NCH))
+        @pl.when(has_next & (piece < NX))
         def _():
             j_copy(piece).wait_recv()
 
-        at = pl.multiple_of(jnp.minimum(c, NCH - 1) * CH, CH)
-        j32[8 : 8 + HALF, pl.ds(at + PAD, CH)] = jb[:, pl.ds(at, CH)].astype(F32)
+        at = pl.multiple_of(jnp.minimum(piece, NX - 1) * CX, CX)
+        j32[8 : 8 + LOW, pl.ds(at + PAD, CX)] = jb[:, pl.ds(at, CX)].astype(F32)
 
     arrive(jnp.int32(0))
-    cross(both, arrive)
+
+    @pl.when(k > 0)
+    def _():
+        cross(True)
+
+    @pl.when(k == 0)
+    def _():
+        cross(False)
 
     bds[0:8, :] = 0.5 * jnp.where(first, bdacc[0:8], bdacc[16:24])
     bhs[0:8, :] = 0.5 * jnp.where(first, bdacc[8:16], bdacc[24:32])
-    bds[8:16, :] = fold(dsums[0], dsums[1])
-    bhs[8:16, :] = fold(dsums[2], dsums[3])
+    tuck(bds, 6, dsums[0], dsums[1])
+    tuck(bhs, 0, dsums[2], dsums[3])
 
     def bo_copy(to, slot):
         return remote(bds, bdo.at[slot], s_bo, r_bo, k, to)
@@ -572,11 +624,15 @@
 
     bdo[s] = bds[...]
 
+    @pl.loop(1, NQ)
+    def _(d):
+        gb_copy(lax.rem(s + d, NQ), s).start()
+
+
     def all_of(ref, n, ss, rs):
         return remote(ref.at[pl.ds(0, n)], ref.at[pl.ds(0, n)], ss, rs, k, lax.rem(s + 1, NQ))
 
     all_of(bm, NQ - 1, s_bm, r_bm).wait_recv()
-    all_of(gall, NQ - 1, s_g, r_g).wait_recv()
 
     row = lax.broadcasted_iota(jnp.int32, (GRID, 128), 0)
 
@@ -587,26 +643,6 @@
         odd = jnp.where(row >= 2, pltpu.roll(odd, 2, 0), 0.0)
         return even + odd
 
-    for i in range(12):
-        for m in range(8):
-            a = gall[2 * m, 8 * i : 8 * i + 8, :]
-            b = gall[2 * m + 1, 8 * i : 8 * i + 8, :]
-            pair = (
-                jnp.where(quarter < 4, a, pltpu.roll(b, 4, 0)),
-                jnp.where(quarter < 4, pltpu.roll(a, 4, 0), b),
-            )
-            for j in range(2):
-                di, h, which = (2 * i + j) // 6, ((2 * i + j) // 3) % 2, (2 * i + j) % 3
-                v = pair[j]
-                if di and m == 7:
-                    v = jnp.where(quarter < 8 - di, v, 0.0)
-                m8 = slice(8 * m, 8 * m + 8)
-                if which < 2:
-                    ga[4 * di + 2 * h + which, m8, :] = v
-                else:
-                    o = swap(v)
-                    gx[4 * di + 2 * h, m8, :] = jnp.where(first, v, o)
-                    gx[4 * di + 2 * h + 1, m8, :] = jnp.where(first, o, v)
     b_i = merge([bm[p, 0:8, :] for p in range(NQ)])
     b_1 = merge([bm[p, 8:16, :] for p in range(NQ)])
 
@@ -625,12 +661,23 @@
     def _():
         all_of(bdh, NQ, s_bh, r_bh).wait_recv()
 
-    b_f = b_i + merge([bdo[p, 0:8, :] + bdh[p, 0:8, :] for p in range(NQ)])
-    tot = bdo[0, 8:16, :] + bdh[0, 8:16, :]
-    for p in range(1, NQ):
-        tot = tot + bdo[p, 8:16, :] + bdh[p, 8:16, :]
-    sum_f = sum_i + total(tot[0:1])
-    sum_fi = sum_ii + total(tot[1:2])
+    @pl.when(k == 0)
+    def _():
+        all_of(bdh, NQ - 1, s_ba, r_bh).wait_recv()
+
+    parts = []
+    tot_d = None
+    tot_di = None
+    for p in range(NQ):
+        up, dn = bdo[p], bdh[p]
+        parts.append(jnp.where(quarter < 6, up, 0.0) + jnp.where((quarter >= 2) | (k == 0), dn, 0.0))
+        a = up[6:7] + jnp.where(k == 0, 0.0, dn[0:1])
+        b = up[7:8] + jnp.where(k == 0, 0.0, dn[1:2])
+        tot_d = a if p == 0 else tot_d + a
+        tot_di = b if p == 0 else tot_di + b
+    b_f = b_i + merge(parts)
+    sum_f = sum_i + total(tot_d)
+    sum_fi = sum_ii + total(tot_di)
     mean_f = sum_f * (1.0 / PIXELS)
 
     def apply_gram(c):
@@ -712,6 +759,33 @@
 
     c = rate * direction(None)
     exchange(0, c)
+
+    all_of(gf, NQ - 1, s_g.at[0], r_g.at[0]).wait_recv()
+    all_of(gb, NQ - 1, s_g.at[1], r_g.at[1]).wait_recv()
+    for m in range(8):
+        ab_f = [gf[2 * m + j] for j in range(2)]
+        ab_b = [gb[2 * m + j].astype(F32) for j in range(2)]
+        for i in range(12):
+            src = ab_f if i < 3 else ab_b
+            o = 8 * i if i < 3 else 8 * (i - 3)
+            a, b = src[0][o : o + 8], src[1][o : o + 8]
+            pair = (
+                jnp.where(quarter < 4, a, pltpu.roll(b, 4, 0)),
+                jnp.where(quarter < 4, pltpu.roll(a, 4, 0), b),
+            )
+            for j in range(2):
+                (di, h), which = order[(2 * i + j) // 3], (2 * i + j) % 3
+                v = pair[j]
+                if di and m == 7:
+                    v = jnp.where(quarter < 8 - di, v, 0.0)
+                m8 = slice(8 * m, 8 * m + 8)
+                if which < 2:
+                    ga[4 * di + 2 * h + which, m8, :] = v
+                else:
+                    o2 = swap(v)
+                    gx[4 * di + 2 * h, m8, :] = jnp.where(first, v, o2)
+                    gx[4 * di + 2 * h + 1, m8, :] = jnp.where(first, o2, v)
+
     for i in range(1, ITERATIONS - 1):
         step = c + rate * direction(c)
         receive(i - 1)
@@ -776,10 +850,10 @@
     mixed_y = jnp.where(big_first, 0.0, mixed).astype(BF16)
     dims = (((1,), (1,)), ((), ()))
 
-    @pl.loop(0, NCH // 4)
+    @pl.loop(0, NCH // 8)
     def _(p):
-        for u in range(4):
-            at = pl.multiple_of((4 * p + u) * CH, CH)
+        for u in range(8):
+            at = pl.multiple_of((8 * p + u) * CH, CH)
             table = cd[pl.ds(at, CH), :]
             sx = lax.dot_general(mixed_x, table, dims, preferred_element_type=F32)
             sy = lax.dot_general(mixed_y, table, dims, preferred_element_type=F32)
@@ -808,15 +882,14 @@
         mid_prev.wait_send()
         bot_prev.wait_send()
 
-    half = sec.at[0, pl.ds(0, HALF)]
 
     @pl.when(has_next)
     def _():
-        remote(half, fb, s_f, r_f.at[0], jnp.minimum(k + 1, NC - 1), s).wait_send()
+        remote(sec.at[0, pl.ds(0, UP)], fb, s_f, r_f.at[0], jnp.minimum(k + 1, NC - 1), s).wait_send()
 
     @pl.when(has_prev)
     def _():
-        remote(half, jb, s_j, r_j.at[0], jnp.maximum(k - 1, 0), s).wait_send()
+        remote(sec.at[0, pl.ds(UP, LOW)], jb, s_j, r_j.at[0], jnp.maximum(k - 1, 0), s).wait_send()
 
     @pl.when(s < NQ - 1)
     def _():
@@ -830,9 +903,15 @@
     def _():
         all_of(bdh, NQ, s_bh, r_bh).wait_send()
 
-    all_of(gall, NQ - 1, s_g, r_g).wait_send()
+    all_of(gf, NQ - 1, s_g.at[0], r_g.at[0]).wait_send()
+    all_of(gb, NQ - 1, s_g.at[1], r_g.at[1]).wait_send()
     all_of(bm, NQ - 1, s_bm, r_bm).wait_send()
     all_of(bdo, NQ - 1, s_bo, r_bo).wait_send()
+
+    @pl.when(k == 0)
+    def _():
+        all_of(bdh, NQ - 1, s_ba, r_bh).wait_send()
+
     all_of(tw, NQ - 1, s_tw, r_tw).wait_send()
 
     for i in range(ITERATIONS - 1):
@@ -857,26 +936,27 @@
         v = pltpu.VMEM
         dma = pltpu.SemaphoreType.DMA
         row = v((1, COLS), F32)
-        win = v((NQ, 16, 128), F32)
+        win = v((NQ, 8, 128), F32)
         scratch = [
-            v((ROWS, COLS), BF16), v((HALF, COLS), BF16), v((HALF, COLS), BF16), v((HALF, COLS), BF16),
-            v((ROWS + 16, COLS + 2 * PAD), F32), v((HALF + 16, COLS + 2 * PAD), F32),
+            v((ROWS, COLS), BF16), v((UP, COLS), BF16), v((LOW, COLS), BF16), v((LOW, COLS), BF16),
+            v((ROWS + 16, COLS + 2 * PAD), F32), v((LOW + 16, COLS + 2 * PAD), F32),
             v((ROWS, COLS), F32), v((ROWS, COLS), F32),
             v((COLS, 128), BF16), v((COLS, 256), BF16),
             v((3, 80, ROWS), BF16), v((32, ROWS), BF16), v((ROWS, 128), BF16),
-            v((2, 5, ROWS, CH), BF16), v((2, 96, CH), BF16), v((96, CH), F32),
+            v((CH, 256), F32), v((2, 5, ROWS, CH), BF16), v((2, 96, CH), BF16), v((96, CH), F32),
             v((2, 2, ROWS, CH), BF16), v((2, 64, CH), BF16),
             v((32, COLS + 2 * PAD), F32), v((64, COLS), BF16), v((32, 128), F32),
             v((2, 8, 128), F32), v((4, 8, 128), F32),
             row, row, row, row, row, row, row,
-            v((96, 128), F32), v((2, 96, 128), F32), v((96, 128), F32), v((NQ, 96, 128), F32),
+            v((96, 128), F32), v((2, 96, 128), F32), v((96, 128), F32), v((96, 128), F32),
+            v((24, 128), F32), v((80, 128), BF16), v((NQ, 24, 128), F32), v((NQ, 80, 128), BF16),
             v((16, GRID, 128), F32), v((16, GRID, 128), F32),
-            v((24, 128), F32), v((NQ, 24, 128), F32), v((16, 128), F32), v((16, 128), F32), win, win,
+            v((24, 128), F32), v((NQ, 24, 128), F32), v((8, 128), F32), v((8, 128), F32), v((8, 128), F32), win, win,
             v((GRID + 16, 128), F32), v((3, GRID, 128), F32), v((3, GRID, 128), F32), v((3, GRID, 128), F32),
             v((8, 128), F32), v((NC - 1, 8, 128), F32), v((8, 128), F32), v((NQ, 8, 128), F32),
             dma((4,)), dma((4,)), dma((2,)), pltpu.SemaphoreType.REGULAR((4,)),
             dma, dma((NX,)), dma, dma((NX,)), dma((4,)), dma((4,)), dma((2,)), dma((2,)),
-            dma, dma, dma, dma, dma, dma, dma, dma,
+            dma((2,)), dma((2,)), dma, dma, dma, dma, dma, dma, dma,
             dma((3,)), dma((3,)), dma((3,)), dma((3,)), dma((NC,)), dma((NC,)), dma, dma,
         ]
         anywhere = pl.BlockSpec(memory_space=pl.ANY)

time: 52 us -> 45.9 us (0.88)
  Pallas kernels: 49.2 us -> 43.2 us
    pallas_call x1, Pallas kernels: 49.2 us -> 43.2 us  [body(): pl.pallas_call(kernel, out_shape=(pltpu.VMEM((1, ROWS, COLS), BF16), pltp...]
where the time goes in v2:
time: 45.9 us; the launch traced here: 45.7 us
  Pallas kernels  43.2 us (94%)
  local copies, waits for them, and re-layouts  1.94 us (4%)
  between operations  0.64 us (1%)
    pallas_call x1, Pallas kernels, body(): pl.pallas_call(kernel, out_shape=(pltpu.VMEM((1, ROWS, COLS), BF16), pltp...  43.2 us
    unnamed x2, local copies, waits for them, and re-layouts  1.94 us

profile of v2, /device:TPU:6, one launch (start us, length us, event | category | flops | bytes accessed | tf_op | source)
XLA Modules:
  0.0 45.7 jit_solution(13128089182691410455)
XLA Ops:
  0.6 43.2 %shard_map.77 = (bf16[1,256,4096]{2,1,0:T(8,128)(2,1)S(1)}, f32[1,64,128]{2,1,0:T(8,128)S(1)}) custom-call(bf16[1,256,4096]{2,1,0:T(8,128)(2,1)} %sec.1, bf16[256,4096]{1,0:T(8,128)(2,1)} %anc.1, bf16[4096,128]{1,0:T(8,128)(2,1)} %constant.8.clone.cd_in, bf16[3,80,256]{2,1,0:T(8,128)(2,1)} %constant.9.clone.rt_in, bf16[32,256]{1,0:T(8,128)(2,1)} %constant.10.clone.sp_in, ...), custom_call_target="tpu_custom_call" | custom-call | tf_op jit(solution)/shard_map/pallas_call | solution.py:964
  43.8 1.3 %copy.10 = bf16[1,256,4096]{2,1,0:T(8,128)(2,1)} copy(bf16[1,256,4096]{2,1,0:T(8,128)(2,1)S(1)} %get-tuple-element.2) | data formatting | bytes 4194304
  45.1 0.6 %copy.11 = f32[1,64,128]{2,1,0:T(8,128)} copy(f32[1,64,128]{2,1,0:T(8,128)S(1)} %get-tuple-element.3) | data formatting | bytes 65536

commit v3 on v2

--- a/solution.py
+++ b/solution.py
@@ -22,6 +22,7 @@
 NCH = COLS // CH
 CX = 512
 NX = COLS // CX
+HOOK = 3
 PAD = 128
 NC = 8
 NQ = 16
@@ -81,7 +82,7 @@
     ib, fb, jb, ab, i32, j32, lxb, lyb, cd, w1, rt, sp, mx,
     wb, qb, tb, gacc, qd, vb, ub, lhs, bdacc, sums, dsums,
     etop, ebot, emid, htop, hbot, jmid, jbot,
-    gs, gn, gp, gt, gfs, gbs, gf, gb, ga, gx, bms, bm, bds, bhs, baa, bdo, bdh,
+    gs, gn, gp, gt, gfs, gbs, gb2s, gf, gb, gb2, ga, gx, bms, bm, bds, bhs, baa, bdo, bdh,
     cpad, csend, cprev, cnext, ew_s, ew, tw_s, tw,
     sem_in, sem_c, sem_a, rounds,
     s_f, r_f, s_j, r_j, s_h, r_h, s_n, r_n, s_g, r_g, s_bm, r_bm,
@@ -98,14 +99,15 @@
             device_id={"chain": kk, "quad": qq}, device_id_type=MESH,
         )
 
-    def in_copy(c):
-        w = COLS // 4
-        return pltpu.make_async_copy(
-            sec.at[0, :, pl.ds(c * w, w)], ib.at[:, pl.ds(c * w, w)], sem_in.at[c]
-        )
-
-    for c in range(4):
-        in_copy(c).start()
+    edge_rows = [(0, 16), (UP - 16, 16), (ROWS - 16, 16)]
+    inner_rows = [(16, UP - 32), (UP, LOW - 16)]
+
+    def in_copy(i):
+        at, n = (edge_rows + inner_rows)[i]
+        return pltpu.make_async_copy(sec.at[0, pl.ds(at, n)], ib.at[pl.ds(at, n)], sem_in.at[i])
+
+    for i in range(3):
+        in_copy(i).start()
     consts = [
         pltpu.make_async_copy(cd_in, cd, sem_c.at[0]),
         pltpu.make_async_copy(rt_in, rt, sem_c.at[1]),
@@ -114,6 +116,8 @@
     ]
     for d in consts:
         d.start()
+    for i in range(3, 5):
+        in_copy(i).start()
     anc_copies = [
         pltpu.make_async_copy(anc.at[pl.ds(0, UP)], fb, sem_a.at[0]),
         pltpu.make_async_copy(anc.at[pl.ds(UP, LOW)], ab, sem_a.at[1]),
@@ -126,25 +130,44 @@
 
     barrier = pltpu.get_barrier_semaphore()
 
-    def hello(sem, step):
+    qz = lax.div(s, 4)
+    qy = lax.rem(s, 4)
+
+    def greet(sem, q):
+        pl.semaphore_signal(sem, inc=1, device_id={"chain": k, "quad": q}, device_id_type=MESH)
+
+    def hello_quad(sem):
+        for d in (1, 3):
+            greet(sem, 4 * qz + lax.rem(qy + d, 4))
+            greet(sem, 4 * lax.rem(qz + d, 4) + qy)
+
+    far_next = (qy == 3) & (s < NQ - 1)
+    far_prev = (qy == 0) & (s > 0)
+
+    def hello_chain(sem, step):
         for sign in (1, -1):
             kk = k + sign * step
-            pl.semaphore_signal(
-                sem, inc=1, device_id={"chain": k, "quad": lax.rem(s + sign * step + NQ, NQ)}, device_id_type=MESH
-            )
 
             @pl.when((kk >= 0) & (kk < NC))
             def _():
                 pl.semaphore_signal(sem, inc=1, device_id={"chain": kk, "quad": s}, device_id_type=MESH)
 
-    def heard(sem, step):
+    def on_chain(step):
         one = jnp.int32(1)
         zero = jnp.int32(0)
-        pl.semaphore_wait(
-            sem, 2 + jnp.where(k >= step, one, zero) + jnp.where(k + step < NC, one, zero)
-        )
-
-    hello(barrier, 1)
+        return jnp.where(k >= step, one, zero) + jnp.where(k + step < NC, one, zero)
+
+    hello_quad(barrier)
+
+    @pl.when(far_next)
+    def _():
+        greet(barrier, s + 1)
+
+    @pl.when(far_prev)
+    def _():
+        greet(barrier, s - 1)
+
+    hello_chain(barrier, 1)
 
     i32[:, :PAD] = jnp.zeros((ROWS + 16, PAD), F32)
     i32[:, PAD + COLS :] = jnp.zeros((ROWS + 16, PAD), F32)
@@ -188,8 +211,9 @@
         def _():
             ew[j] = jnp.zeros((8, 128), F32)
 
-    heard(barrier, 1)
-    hello(rounds.at[0], 1)
+    far = jnp.where(far_next, jnp.int32(1), jnp.int32(0)) + jnp.where(far_prev, jnp.int32(1), jnp.int32(0))
+    pl.semaphore_wait(barrier, 4 + far + on_chain(1))
+    hello_quad(rounds.at[0])
 
     def f_copy(c):
         at = pl.multiple_of(c * CX, CX)
@@ -220,8 +244,8 @@
     mid_prev = remote(emid, jmid, s_h.at[2], r_h.at[2], jnp.maximum(k - 1, 0), s)
     bot_prev = remote(hbot, jbot, s_h.at[3], r_h.at[3], jnp.maximum(k - 1, 0), s)
 
-    for c in range(4):
-        in_copy(c).wait()
+    for i in range(3):
+        in_copy(i).wait()
     etop[...] = ib[0:16, :].astype(F32)[0:1]
     ebot[...] = ib[ROWS - 16 : ROWS, :].astype(F32)[15:16]
     emid[...] = ib[UP - 16 : UP, :].astype(F32)[15:16]
@@ -265,6 +289,12 @@
 
     def spot(c):
         return pl.multiple_of(jnp.maximum(c, 0) * CH, CH)
+
+    for i in range(3, 5):
+        in_copy(i).wait()
+
+    pl.semaphore_wait(rounds.at[0], 4)
+    hello_quad(rounds.at[1])
 
     @pl.loop(0, NCH // 2)
     def _(p):
@@ -300,8 +330,8 @@
     i32[7:8, PAD : PAD + COLS] = htop[...]
     i32[8 + ROWS : 9 + ROWS, PAD : PAD + COLS] = hbot[...]
 
-    heard(rounds.at[0], 1)
-    hello(rounds.at[1], 2)
+    pl.semaphore_wait(rounds.at[1], 4)
+    hello_quad(rounds.at[2])
 
     def tally(i, d, x):
         a = jnp.zeros((8, CH), F32)
@@ -363,15 +393,10 @@
     def own_pass(with_anchor):
         @pl.loop(0, NCH // 2)
         def _(p):
-            @pl.when(p == 3)
+            @pl.when(p == 5)
             def _():
-                heard(rounds.at[1], 2)
-                hello(rounds.at[2], 4)
-
-            @pl.when(p == 7)
-            def _():
-                heard(rounds.at[2], 4)
-                hello(rounds.at[3], 1)
+                pl.semaphore_wait(rounds.at[2], 4)
+                hello_chain(rounds.at[3], 1)
 
             for u in range(2):
                 c = 2 * p + u
@@ -463,13 +488,14 @@
     def _(d):
         bm_copy(lax.rem(s + d, NQ), s).start()
 
-    heard(rounds.at[3], 1)
-
     def gf_copy(to, slot):
         return remote(gfs, gf.at[slot], s_g.at[0], r_g.at[0], k, to)
 
     def gb_copy(to, slot):
         return remote(gbs, gb.at[slot], s_g.at[1], r_g.at[1], k, to)
+
+    def gb2_copy(to, slot):
+        return remote(gb2s, gb2.at[slot], s_g.at[2], r_g.at[2], k, to)
 
     def spread_gram():
         @pl.when(s > 0)
@@ -485,8 +511,9 @@
             b8 = slice(8 * i, 8 * i + 8)
             gt[b8, :] = gs[b8, :] + jnp.where(lower_rows, gn[0, b8, :], gn[1, b8, :])
         gfs[...] = gt[0:24, :]
-        gbs[0:64, :] = gt[24:88, :].astype(BF16)
-        gbs[64:80, :] = jnp.concatenate([gt[88:96, :], jnp.zeros((8, 128), F32)], axis=0).astype(BF16)
+        gbs[...] = gt[24:72, :].astype(BF16)
+        gb2s[...] = jnp.concatenate([gt[72:96, :], jnp.zeros((8, 128), F32)], axis=0).astype(BF16)
+        gb2[s] = gb2s[...]
         gf[s] = gfs[...]
         gb[s] = gbs[...]
 
@@ -549,7 +576,7 @@
     def cross(upper):
         @pl.loop(0, NCH // 2)
         def _(p):
-            @pl.when(p == 2)
+            @pl.when(p == HOOK)
             def _():
                 spread_gram()
 
@@ -610,6 +637,9 @@
     def bh_copy(to, slot):
         return remote(bhs, bdh.at[slot], s_bh, r_bh, jnp.minimum(k + 1, NC - 1), to)
 
+    pl.semaphore_wait(rounds.at[3], on_chain(1))
+    hello_chain(rounds.at[4], 2)
+
     @pl.loop(0, NQ)
     def _(d):
         to = lax.rem(s + d, NQ)
@@ -627,6 +657,7 @@
     @pl.loop(1, NQ)
     def _(d):
         gb_copy(lax.rem(s + d, NQ), s).start()
+        gb2_copy(lax.rem(s + d, NQ), s).start()
 
 
     def all_of(ref, n, ss, rs):
@@ -760,11 +791,17 @@
     c = rate * direction(None)
     exchange(0, c)
 
+    pl.semaphore_wait(rounds.at[4], on_chain(2))
+    hello_chain(rounds.at[5], 4)
+
     all_of(gf, NQ - 1, s_g.at[0], r_g.at[0]).wait_recv()
     all_of(gb, NQ - 1, s_g.at[1], r_g.at[1]).wait_recv()
+    all_of(gb2, NQ - 1, s_g.at[2], r_g.at[2]).wait_recv()
     for m in range(8):
         ab_f = [gf[2 * m + j] for j in range(2)]
-        ab_b = [gb[2 * m + j].astype(F32) for j in range(2)]
+        ab_b = [
+            jnp.concatenate([gb[2 * m + j].astype(F32), gb2[2 * m + j].astype(F32)], axis=0) for j in range(2)
+        ]
         for i in range(12):
             src = ab_f if i < 3 else ab_b
             o = 8 * i if i < 3 else 8 * (i - 3)
@@ -805,6 +842,8 @@
     mine = window(step) - jnp.where(k == 0, SMOOTHING, 0.0) * cw
     ew_s[...] = mine
 
+    pl.semaphore_wait(rounds.at[5], on_chain(4))
+
     def ew_copy(to, slot):
         return remote(ew_s, ew.at[slot], s_ew.at[to], r_ew.at[slot], to, s)
 
@@ -905,6 +944,7 @@
 
     all_of(gf, NQ - 1, s_g.at[0], r_g.at[0]).wait_send()
     all_of(gb, NQ - 1, s_g.at[1], r_g.at[1]).wait_send()
+    all_of(gb2, NQ - 1, s_g.at[2], r_g.at[2]).wait_send()
     all_of(bm, NQ - 1, s_bm, r_bm).wait_send()
     all_of(bdo, NQ - 1, s_bo, r_bo).wait_send()
 
@@ -949,14 +989,15 @@
             v((2, 8, 128), F32), v((4, 8, 128), F32),
             row, row, row, row, row, row, row,
             v((96, 128), F32), v((2, 96, 128), F32), v((96, 128), F32), v((96, 128), F32),
-            v((24, 128), F32), v((80, 128), BF16), v((NQ, 24, 128), F32), v((NQ, 80, 128), BF16),
+            v((24, 128), F32), v((48, 128), BF16), v((32, 128), BF16),
+            v((NQ, 24, 128), F32), v((NQ, 48, 128), BF16), v((NQ, 32, 128), BF16),
             v((16, GRID, 128), F32), v((16, GRID, 128), F32),
             v((24, 128), F32), v((NQ, 24, 128), F32), v((8, 128), F32), v((8, 128), F32), v((8, 128), F32), win, win,
             v((GRID + 16, 128), F32), v((3, GRID, 128), F32), v((3, GRID, 128), F32), v((3, GRID, 128), F32),
             v((8, 128), F32), v((NC - 1, 8, 128), F32), v((8, 128), F32), v((NQ, 8, 128), F32),
-            dma((4,)), dma((4,)), dma((2,)), pltpu.SemaphoreType.REGULAR((4,)),
+            dma((5,)), dma((4,)), dma((2,)), pltpu.SemaphoreType.REGULAR((6,)),
             dma, dma((NX,)), dma, dma((NX,)), dma((4,)), dma((4,)), dma((2,)), dma((2,)),
-            dma((2,)), dma((2,)), dma, dma, dma, dma, dma, dma, dma,
+            dma((3,)), dma((3,)), dma, dma, dma, dma, dma, dma, dma,
             dma((3,)), dma((3,)), dma((3,)), dma((3,)), dma((NC,)), dma((NC,)), dma, dma,
         ]
         anywhere = pl.BlockSpec(memory_space=pl.ANY)

time: 45.9 us -> 44.8 us (0.976)
  Pallas kernels: 43.2 us -> 42.1 us
    pallas_call x1, Pallas kernels: 43.2 us -> 42.1 us  [body(): pl.pallas_call(kernel, out_shape=(pltpu.VMEM((1, ROWS, COLS), BF16), pltp...]
where the time goes in v3:
time: 44.8 us; the launch traced here: 44.7 us
  Pallas kernels  42.1 us (94%)
  local copies, waits for them, and re-layouts  1.94 us (4%)
  between operations  0.64 us (1%)
    pallas_call x1, Pallas kernels, body(): pl.pallas_call(kernel, out_shape=(pltpu.VMEM((1, ROWS, COLS), BF16), pltp...  42.1 us
    unnamed x2, local copies, waits for them, and re-layouts  1.94 us

profile of v3, /device:TPU:6, one launch (start us, length us, event | category | flops | bytes accessed | tf_op | source)
XLA Modules:
  0.0 44.7 jit_solution(17860526629233253732)
XLA Ops:
  0.6 42.1 %shard_map.77 = (bf16[1,256,4096]{2,1,0:T(8,128)(2,1)S(1)}, f32[1,64,128]{2,1,0:T(8,128)S(1)}) custom-call(bf16[1,256,4096]{2,1,0:T(8,128)(2,1)} %sec.1, bf16[256,4096]{1,0:T(8,128)(2,1)} %anc.1, bf16[4096,128]{1,0:T(8,128)(2,1)} %constant.8.clone.cd_in, bf16[3,80,256]{2,1,0:T(8,128)(2,1)} %constant.9.clone.rt_in, bf16[32,256]{1,0:T(8,128)(2,1)} %constant.10.clone.sp_in, ...), custom_call_target="tpu_custom_call" | custom-call | tf_op jit(solution)/shard_map/pallas_call | solution.py:1005
  42.8 1.3 %copy.10 = bf16[1,256,4096]{2,1,0:T(8,128)(2,1)} copy(bf16[1,256,4096]{2,1,0:T(8,128)(2,1)S(1)} %get-tuple-element.2) | data formatting | bytes 4194304
  44.1 0.6 %copy.11 = f32[1,64,128]{2,1,0:T(8,128)} copy(f32[1,64,128]{2,1,0:T(8,128)S(1)} %get-tuple-element.3) | data formatting | bytes 65536

commit v4 on v3

--- a/solution.py
+++ b/solution.py
@@ -141,6 +141,11 @@
             greet(sem, 4 * qz + lax.rem(qy + d, 4))
             greet(sem, 4 * lax.rem(qz + d, 4) + qy)
 
+    def others():
+        hops = lambda d: min(d, 4 - d)
+        steps = sorted(((z, y) for z in range(4) for y in range(4) if z or y), key=lambda t: -hops(t[0]) - hops(t[1]))
+        return [4 * lax.rem(qz + z, 4) + lax.rem(qy + y, 4) for z, y in steps]
+
     far_next = (qy == 3) & (s < NQ - 1)
     far_prev = (qy == 0) & (s > 0)
 
@@ -517,9 +522,7 @@
         gf[s] = gfs[...]
         gb[s] = gbs[...]
 
-        @pl.loop(1, NQ)
-        def _(d):
-            to = lax.rem(s + d, NQ)
+        for to in others():
             gf_copy(to, s).start()
 
     @pl.when(has_next)
@@ -640,24 +643,22 @@
     pl.semaphore_wait(rounds.at[3], on_chain(1))
     hello_chain(rounds.at[4], 2)
 
-    @pl.loop(0, NQ)
-    def _(d):
-        to = lax.rem(s + d, NQ)
-
+    for to in others():
         @pl.when(has_next)
         def _():
             bh_copy(to, s).start()
 
-        @pl.when(d > 0)
-        def _():
-            bo_copy(to, s).start()
+        bo_copy(to, s).start()
+
+    @pl.when(has_next)
+    def _():
+        bh_copy(s, s).start()
 
     bdo[s] = bds[...]
 
-    @pl.loop(1, NQ)
-    def _(d):
-        gb_copy(lax.rem(s + d, NQ), s).start()
-        gb2_copy(lax.rem(s + d, NQ), s).start()
+    for to in others():
+        gb_copy(to, s).start()
+        gb2_copy(to, s).start()
 
 
     def all_of(ref, n, ss, rs):
@@ -847,7 +848,7 @@
     def ew_copy(to, slot):
         return remote(ew_s, ew.at[slot], s_ew.at[to], r_ew.at[slot], to, s)
 
-    for kk in range(1, NC):
+    for kk in range(NC - 1, 0, -1):
         @pl.when(kk > k)
         def _():
             ew_copy(kk, k).start()
@@ -870,9 +871,8 @@
     def tw_copy(to, slot):
         return remote(tw_s, tw.at[slot], s_tw, r_tw, k, to)
 
-    @pl.loop(1, NQ)
-    def _(d):
-        tw_copy(lax.rem(s + d, NQ), s).start()
+    for to in others():
+        tw_copy(to, s).start()
 
     tw[s] = t
 

time: 44.8 us -> 44.1 us (0.984)
  Pallas kernels: 42.1 us -> 41.5 us
    pallas_call x1, Pallas kernels: 42.1 us -> 41.5 us  [body(): pl.pallas_call(kernel, out_shape=(pltpu.VMEM((1, ROWS, COLS), BF16), pltp...]
where the time goes in v4:
time: 44.1 us; the launch traced here: 44 us
  Pallas kernels  41.5 us (94%)
  local copies, waits for them, and re-layouts  1.94 us (4%)
  between operations  0.64 us (1%)
    pallas_call x1, Pallas kernels, body(): pl.pallas_call(kernel, out_shape=(pltpu.VMEM((1, ROWS, COLS), BF16), pltp...  41.5 us
    unnamed x2, local copies, waits for them, and re-layouts  1.94 us

profile of v4, /device:TPU:6, one launch (start us, length us, event | category | flops | bytes accessed | tf_op | source)
XLA Modules:
  0.0 44.0 jit_solution(17427284229221943502)
XLA Ops:
  0.6 41.5 %shard_map.77 = (bf16[1,256,4096]{2,1,0:T(8,128)(2,1)S(1)}, f32[1,64,128]{2,1,0:T(8,128)S(1)}) custom-call(bf16[1,256,4096]{2,1,0:T(8,128)(2,1)} %sec.1, bf16[256,4096]{1,0:T(8,128)(2,1)} %anc.1, bf16[4096,128]{1,0:T(8,128)(2,1)} %constant.8.clone.cd_in, bf16[3,80,256]{2,1,0:T(8,128)(2,1)} %constant.9.clone.rt_in, bf16[32,256]{1,0:T(8,128)(2,1)} %constant.10.clone.sp_in, ...), custom_call_target="tpu_custom_call" | custom-call | tf_op jit(solution)/shard_map/pallas_call | solution.py:1005
  42.1 1.3 %copy.10 = bf16[1,256,4096]{2,1,0:T(8,128)(2,1)} copy(bf16[1,256,4096]{2,1,0:T(8,128)(2,1)S(1)} %get-tuple-element.2) | data formatting | bytes 4194304
  43.4 0.6 %copy.11 = f32[1,64,128]{2,1,0:T(8,128)} copy(f32[1,64,128]{2,1,0:T(8,128)S(1)} %get-tuple-element.3) | data formatting | bytes 65536
